TPU v7x, 32 devices: a whole 2x2x4 slice. The times are simulated.
32 devices in a mesh: gx: 8 (over y, x, core), gy: 4 (over z).
Axes of the slice: x: 2, y: 2, z: 4, core: 2. Of those that a mesh axis runs over, the one named last changes fastest.
Arguments:
- products: bfloat16 [1536, 3, 2048], P('gy', None, 'gx'), may hold values from -6 to 6
- operator: bfloat16 [1536, 1536], P(None, 'gy'), may hold values from -0.21875 to 0.21875
Outputs:
- derivative: bfloat16 [1536, 3, 2048], P(('gy', 'gx'))
All inputs are finite; a program needn't handle non-finite values.
Results may differ from a plain program's by a relative error of at most 0.002.
Values may be sent and summed in bfloat16 or wider, within the bound.
A program may use at most 64 MiB of HBM per device.

v0:
```python
import functools

import jax
import jax.numpy as jnp
from jax import lax
from jax.experimental import pallas as pl
from jax.experimental.pallas import tpu as pltpu
from jax.sharding import PartitionSpec as P

MESH = pl.DeviceIdType.MESH
LANES = 128
SUBLANES = 16
VMEM_BYTES = 60 * 1024 * 1024
GRANT = 54500 * 1024


def kernel(n, g, parts, p_ref, op_ref, out_ref, blocks, ops, res,
           own_send, fwd_send, op_send, spread_send, res_send, blk_recv, op_recv, out_recv, own_copy, ready, ahead_of):
    j, k = lax.axis_index("gx"), lax.axis_index("gy")
    half = n // 2
    side = lax.div(k, half)
    step = 1 - 2 * side
    centre = jnp.where(side == 0, half - 1, half)
    other = n - 1 - centre
    is_centre = k == centre
    planes, rows, cols = p_ref.shape
    width = cols // parts
    chunks = planes * parts
    piece = half * rows // g
    outrows = rows // g
    ahead, lead = 2, chunks - 1

    def flip(mask):
        to = j
        for bit in (1 << b for b in range(mask.bit_length())):
            if mask & bit:
                to = to + bit * (1 - 2 * lax.rem(lax.div(j, bit), 2))
        return to

    def near(d):
        return centre - step * d

    def far(d):
        return other + step * d

    rounds = g.bit_length() - 1
    barrier = pltpu.get_barrier_semaphore()

    def signal(sem, gx, gy):
        pl.semaphore_signal(sem, inc=1, device_id=(gx, gy), device_id_type=MESH)

    for b in range(rounds):
        signal(barrier, flip(1 << b), k)

    @pl.when(is_centre)
    def _():
        signal(barrier, j, other)
        for d in range(1, half):
            signal(barrier, j, near(d))
        pl.semaphore_wait(barrier, rounds + half)

    @pl.when(jnp.logical_not(is_centre))
    def _():
        signal(barrier, j, centre)
        pl.semaphore_wait(barrier, rounds + 1)

    def plane_entered():
        for b in range(rounds):
            signal(ready.at[b], flip(1 << b), k)
            pl.semaphore_wait(ready.at[b], 1)

    def remote(src, dst, send, recv, gx, gy):
        return pltpu.make_async_remote_copy(
            src_ref=src, dst_ref=dst, send_sem=send, recv_sem=recv,
            device_id=(gx, gy), device_id_type=MESH)

    def wait_bytes(ref, sem):
        pltpu.make_async_copy(ref, ref, sem).wait()

    def chunk_of(ref, i):
        c, h = lax.div(i, parts), lax.rem(i, parts)
        return ref.at[c, :, pl.ds(pl.multiple_of(h * width, width), width)]

    def piece_rows(at):
        return pl.ds(pl.multiple_of(at * piece, piece), piece)

    def from_source(s):
        return pl.ds(pl.multiple_of(s * rows, rows), rows)

    def op_part(s, at):
        return ops.at[piece_rows(at), from_source(s)]

    def block_part(s, i):
        c, h = lax.div(i, parts), lax.rem(i, parts)
        return blocks.at[c, from_source(s), pl.ds(pl.multiple_of(h * width, width), width)]

    def op_out(slot, to_side, to):
        at = pl.multiple_of(to_side * (half * rows) + j * piece, piece)
        remote(op_ref.at[pl.ds(at, piece), :], op_part(k, j),
               op_send.at[slot], op_recv.at[k, j], j, to).start()

    def block_out(i, to):
        remote(chunk_of(p_ref, i), block_part(k, i), own_send, blk_recv.at[k, i], j, to).start()

    @pl.when(is_centre)
    def _():
        op_out(0, 1 - side, other)
        for i in range(ahead):
            block_out(i, other)
        for d in range(1, half):
            signal(ready.at[rounds], j, near(d))
        own_rows = pl.ds(pl.multiple_of(side * (half * rows), half * rows), half * rows)
        own_ops = pltpu.make_async_copy(op_ref.at[own_rows, :], ops.at[:, from_source(k)], own_copy.at[0])
        own_ops.start()
        own_blocks = pltpu.make_async_copy(p_ref, blocks.at[:, from_source(k), :], own_copy.at[1])
        own_blocks.start()

        plane_entered()
        pl.semaphore_wait(ready.at[rounds], half - 1)

        sources = [near(d) for d in range(1, half)] + [far(d) for d in range(half)]
        sibling = flip(1)

        def spread(s, at, to):
            part = op_part(s, at)
            remote(part, part, spread_send.at[s], op_recv.at[s, at], to, k).start()

        def arrived(s, at):
            part = op_part(s, at)
            wait_bytes(part, op_recv.at[s, at])

        for s in sources:
            arrived(s, j)
            for d in range(1, g // 2):
                spread(s, j, flip(2 * d))
            spread(s, j, sibling)
        def forward(i):
            for d in range(1, half):
                part = block_part(near(d), i)
                wait_bytes(part, blk_recv.at[near(d), i])
                remote(part, part, fwd_send.at[d - 1], blk_recv.at[near(d), i], j, other).start()

        for i in range(lead):
            forward(i)
            if i + ahead < lead:
                block_out(i + ahead, other)
        block_out(lead, other)
        for s in sources:
            for d in range(1, g // 2):
                at = flip(2 * d)
                arrived(s, at)
                spread(s, at, sibling)
        for s in sources:
            for d in range(g // 2):
                arrived(s, flip(2 * d + 1))
        own_ops.wait()
        own_blocks.wait()

        def one(i, carry):
            c, h = lax.div(i, parts), lax.rem(i, parts)
            lane = pl.ds(pl.multiple_of(h * width, width), width)

            @pl.when(i + lead < chunks)
            def _():
                forward(i + lead)

            last = far(half - 1)
            others = pl.ds(pl.multiple_of(side * rows, rows), (n - 1) * rows)
            for d in range(half - 1):
                wait_bytes(block_part(far(d), i), blk_recv.at[far(d), i])
            ahead_of[...] = jnp.dot(ops[:, others], blocks[c, others, lane], preferred_element_type=jnp.float32)
            wait_bytes(block_part(last, i), blk_recv.at[last, i])
            target = pl.ds(pl.multiple_of(j * cols + h * width, width), width)
            for d in reversed(range(half)):
                rel = pl.multiple_of((near(d) - side * half) * rows, rows)
                total = ahead_of[pl.ds(rel, rows), :] + jnp.dot(
                    ops[pl.ds(rel, rows), from_source(last)], blocks[c, from_source(last), lane],
                    preferred_element_type=jnp.float32)
                res[d, c, :, lane] = total.astype(res.dtype)
                for mask in reversed(range(1 if d == 0 else 0, g)):
                    to = flip(mask)
                    remote(res.at[d, c, pl.ds(pl.multiple_of(to * outrows, outrows), outrows), lane],
                           out_ref.at[c, :, target], res_send.at[d], out_recv, to, near(d)).start()
                if d == 0:
                    pltpu.make_async_copy(
                        res.at[d, c, pl.ds(pl.multiple_of(j * outrows, outrows), outrows), lane],
                        out_ref.at[c, :, target], out_recv).start()
            return carry

        lax.fori_loop(0, chunks, one, 0)
        wait_bytes(op_part(0, 0), op_send.at[0])
        wait_bytes(blocks.at[:, from_source(0), :], own_send)
        for d in range(1, half):
            wait_bytes(blocks.at[:, from_source(0), :], fwd_send.at[d - 1])
        for s in sources:
            wait_bytes(ops.at[pl.ds(0, (g - 1) * piece), from_source(0)], spread_send.at[s])
        for d in range(half):
            sent = rows - outrows if d == 0 else rows
            wait_bytes(res.at[d, :, pl.ds(0, sent), :], res_send.at[d])

    @pl.when(jnp.logical_not(is_centre))
    def _():
        op_out(1, side, centre)
        block_out(0, centre)
        pl.semaphore_wait(ready.at[rounds], 1)
        op_out(0, 1 - side, other)
        for i in range(1, chunks):
            block_out(i, centre)
        plane_entered()
        signal(ready.at[rounds], j, centre)
        wait_bytes(op_part(0, 0), op_send.at[0])
        wait_bytes(op_part(0, 0), op_send.at[1])
        wait_bytes(blocks.at[:, from_source(0), :], own_send)

    wait_bytes(out_ref, out_recv)


def at_centres(n, g, products, operator):
    rows, planes, cols = products.shape
    parts = 2 if cols % (2 * LANES) == 0 else 1
    half = n // 2
    chunks = planes * parts
    out = pl.pallas_call(
        functools.partial(kernel, n, g, parts),
        out_shape=jax.ShapeDtypeStruct((planes, rows // g, cols * g), jnp.bfloat16),
        in_specs=[pl.BlockSpec(memory_space=pl.ANY)] * 2,
        out_specs=pl.BlockSpec(memory_space=pl.ANY),
        scratch_shapes=[
            pltpu.VMEM((planes, n * rows, cols), jnp.bfloat16),
            pltpu.VMEM((half * rows, n * rows), jnp.bfloat16),
            pltpu.VMEM((half, planes, rows, cols), jnp.bfloat16),
            pltpu.SemaphoreType.DMA,
            pltpu.SemaphoreType.DMA((half,)),
            pltpu.SemaphoreType.DMA((2,)),
            pltpu.SemaphoreType.DMA((n,)),
            pltpu.SemaphoreType.DMA((half,)),
            pltpu.SemaphoreType.DMA((n, chunks)),
            pltpu.SemaphoreType.DMA((n, g)),
            pltpu.SemaphoreType.DMA,
            pltpu.SemaphoreType.DMA((2,)),
            pltpu.SemaphoreType.REGULAR((g.bit_length(),)),
            pltpu.VMEM((half * rows, cols // parts), jnp.float32),
        ],
        compiler_params=pltpu.CompilerParams(
            collective_id=0, has_side_effects=True, vmem_limit_bytes=GRANT),
    )(products.transpose(1, 0, 2), operator)
    return out.transpose(1, 0, 2)


def by_collectives(products, operator):
    y_local, three, m_local = products.shape
    flat = products.reshape(y_local, three * m_local)
    summed = lax.psum_scatter(
        jnp.dot(operator, flat, preferred_element_type=jnp.float32), "gy", scatter_dimension=0, tiled=True)
    result = summed.astype(jnp.bfloat16).reshape(y_local, three, m_local)
    return lax.all_to_all(result, "gx", split_axis=0, concat_axis=2, tiled=True)


def solution(mesh):
    n, g = mesh.shape["gy"], mesh.shape["gx"]

    def body(products, operator):
        rows, planes, cols = products.shape
        aligned = (n % 2 == 0 and planes > 2 and g & (g - 1) == 0 and g > 1 and rows % (g * SUBLANES) == 0
                   and rows % LANES == 0 and cols % LANES == 0)
        held = 2 * (products.size * (n + n // 2 + 2) + operator.size * (1 + n // 2))
        if aligned and held < VMEM_BYTES // 2:
            return at_centres(n, g, products, operator)
        return by_collectives(products, operator)

    return jax.shard_map(
        body,
        mesh=mesh,
        in_specs=(P("gy", None, "gx"), P(None, "gy")),
        out_specs=P(("gy", "gx"), None, None),
        check_vma=False,
    )
```

profile of v0, /device:TPU:0, one launch (start us, length us, event | category | flops | bytes accessed | tf_op | source)
XLA Modules:
  0.0 40.7 jit_solution(11929372791022864675)
XLA Ops:
  0.0 39.9 %shard_map.28 = bf16[3,48,2048]{2,1,0:T(8,128)(2,1)S(1)} custom-call(bf16[3,384,256]{2,1,0:T(8,128)(2,1)} %bitcast.3, bf16[1536,384]{1,0:T(8,128)(2,1)} %op_ref.1), custom_call_target="tpu_custom_call" | custom-call | tf_op jit(solution)/shard_map/pallas_call | solution.py:223
  39.9 0.8 %copy.4 = bf16[48,3,2048]{2,0,1:T(8,128)(2,1)} copy(bf16[48,3,2048]{2,0,1:T(8,128)(2,1)S(1)} %bitcast.2) | data formatting | bytes 1179648
where the time goes:
time: 40.8 us; the launch traced here: 40.7 us
  Pallas kernels  39.9 us (98%)
  local copies, waits for them, and re-layouts  0.82 us (2%)
    pallas_call x1, Pallas kernels, at_centres(): pl.pallas_call(functools.partial(kernel, n, g, parts), out_shape=jax.Shap...  39.9 us
    unnamed x1, local copies, waits for them, and re-layouts  0.82 us

commit v1 on v0

--- a/solution.py
+++ b/solution.py
@@ -15,7 +15,9 @@
 
 
 def kernel(n, g, parts, p_ref, op_ref, out_ref, blocks, ops, res,
-           own_send, fwd_send, op_send, spread_send, res_send, blk_recv, op_recv, out_recv, own_copy, ready, ahead_of):
+           own_send, fwd_send, op_send, spread_send, res_send, blk_recv, op_recv, out_recv, own_copy, ready, ahead_of,
+           op_far, tail, part, part_in, far_terms, near_terms, terms, last,
+           part_send, part_recv, far_send, near_send, terms_recv, last_copy):
     j, k = lax.axis_index("gx"), lax.axis_index("gy")
     half = n // 2
     side = lax.div(k, half)
@@ -28,7 +30,8 @@
     chunks = planes * parts
     piece = half * rows // g
     outrows = rows // g
-    ahead, lead = 2, chunks - 1
+    raw = chunks - 1
+    ahead, lead = 2, min(3, raw)
 
     def flip(mask):
         to = j
@@ -64,6 +67,30 @@
         signal(barrier, j, centre)
         pl.semaphore_wait(barrier, rounds + 1)
 
+    def hops(owner):
+        d, to = owner
+        return bin(to >> 1).count("1") - d, to
+
+    owners = sorted(((d, to) for d in range(half) for to in range(g)), key=hops)
+
+    def far_rows(d, to):
+        rel = far(d) - (1 - side) * half
+        return pl.ds(pl.multiple_of(rel * rows + to * outrows, outrows), outrows)
+
+    def near_rows(d, to):
+        rel = near(d) - side * half
+        return pl.ds(pl.multiple_of(rel * rows + to * outrows, outrows), outrows)
+
+    far_op = pltpu.make_async_copy(
+        op_ref.at[pl.ds(pl.multiple_of((1 - side) * (half * rows), half * rows), half * rows), :], op_far,
+        own_copy.at[2])
+    tail_in = pltpu.make_async_copy(p_ref.at[planes - 1, :, pl.ds((parts - 1) * width, width)], tail, own_copy.at[3])
+
+    def own_part():
+        far_op.wait()
+        tail_in.wait()
+        part[...] = jnp.dot(op_far[...], tail[...], preferred_element_type=jnp.float32)
+
     def plane_entered():
         for b in range(rounds):
             signal(ready.at[b], flip(1 << b), k)
@@ -100,7 +127,7 @@
                op_send.at[slot], op_recv.at[k, j], j, to).start()
 
     def block_out(i, to):
-        remote(chunk_of(p_ref, i), block_part(k, i), own_send, blk_recv.at[k, i], j, to).start()
+        remote(chunk_of(p_ref, i), block_part(k, i), own_send.at[i], blk_recv.at[k, i], j, to).start()
 
     @pl.when(is_centre)
     def _():
@@ -114,9 +141,12 @@
         own_ops.start()
         own_blocks = pltpu.make_async_copy(p_ref, blocks.at[:, from_source(k), :], own_copy.at[1])
         own_blocks.start()
+        far_op.start()
+        tail_in.start()
 
         plane_entered()
         pl.semaphore_wait(ready.at[rounds], half - 1)
+        signal(ready.at[rounds + 1], j, other)
 
         sources = [near(d) for d in range(1, half)] + [far(d) for d in range(half)]
         sibling = flip(1)
@@ -134,17 +164,23 @@
             for d in range(1, g // 2):
                 spread(s, j, flip(2 * d))
             spread(s, j, sibling)
+        own_part()
+
         def forward(i):
             for d in range(1, half):
-                part = block_part(near(d), i)
-                wait_bytes(part, blk_recv.at[near(d), i])
-                remote(part, part, fwd_send.at[d - 1], blk_recv.at[near(d), i], j, other).start()
+                at = block_part(near(d), i)
+                wait_bytes(at, blk_recv.at[near(d), i])
+                remote(at, at, fwd_send.at[d - 1, i], blk_recv.at[near(d), i], j, other).start()
+
+        def step_on(i):
+            forward(i)
+
+            @pl.when(jnp.logical_and(i >= ahead - 1, i + 1 < raw))
+            def _():
+                block_out(i + 1, other)
 
         for i in range(lead):
-            forward(i)
-            if i + ahead < lead:
-                block_out(i + ahead, other)
-        block_out(lead, other)
+            step_on(jnp.int32(i))
         for s in sources:
             for d in range(1, g // 2):
                 at = flip(2 * d)
@@ -156,63 +192,118 @@
         own_ops.wait()
         own_blocks.wait()
 
+        def near_half():
+            lane = pl.ds((parts - 1) * width, width)
+            for d in range(1, half):
+                wait_bytes(block_part(near(d), raw), blk_recv.at[near(d), raw])
+            mine = pl.ds(pl.multiple_of(side * (half * rows), half * rows), half * rows)
+            near_terms[...] = jnp.dot(
+                ops[:, mine], blocks[planes - 1, mine, lane],
+                preferred_element_type=jnp.float32).astype(near_terms.dtype)
+            target = terms.at[1, :, pl.ds(pl.multiple_of(j * width, width), width)]
+            for d in reversed(range(half)):
+                for mask in reversed(range(1 if d == 0 else 0, g)):
+                    to = flip(mask)
+                    remote(near_terms.at[near_rows(d, to), :], target, near_send, terms_recv.at[1],
+                           to, near(d)).start()
+            pltpu.make_async_copy(near_terms.at[near_rows(0, j), :], target, terms_recv.at[1]).start()
+
+        def far_half():
+            target = terms.at[0, :, pl.ds(pl.multiple_of(j * width, width), width)]
+            pl.semaphore_wait(ready.at[rounds + 1], 1)
+            for at, (d, to) in enumerate(owners):
+                band = far_rows(d, to)
+                total = part[band, :]
+                for m in range(half - 1):
+                    wait_bytes(part_in.at[m, band, :], part_recv.at[m, at])
+                    total = total + part_in[m, band, :]
+                far_terms[band, :] = total.astype(far_terms.dtype)
+                remote(far_terms.at[band, :], target, far_send, terms_recv.at[0], to, far(d)).start()
+
         def one(i, carry):
             c, h = lax.div(i, parts), lax.rem(i, parts)
             lane = pl.ds(pl.multiple_of(h * width, width), width)
 
-            @pl.when(i + lead < chunks)
+            @pl.when(i + lead < raw)
             def _():
-                forward(i + lead)
-
-            last = far(half - 1)
+                step_on(i + lead)
+
+            @pl.when(i == raw - 1)
+            def _():
+                near_half()
+                far_half()
+
+            final = far(half - 1)
             others = pl.ds(pl.multiple_of(side * rows, rows), (n - 1) * rows)
             for d in range(half - 1):
                 wait_bytes(block_part(far(d), i), blk_recv.at[far(d), i])
             ahead_of[...] = jnp.dot(ops[:, others], blocks[c, others, lane], preferred_element_type=jnp.float32)
-            wait_bytes(block_part(last, i), blk_recv.at[last, i])
+            wait_bytes(block_part(final, i), blk_recv.at[final, i])
             target = pl.ds(pl.multiple_of(j * cols + h * width, width), width)
+            arrival = out_recv.at[lax.div(c, planes - 1)]
             for d in reversed(range(half)):
                 rel = pl.multiple_of((near(d) - side * half) * rows, rows)
                 total = ahead_of[pl.ds(rel, rows), :] + jnp.dot(
-                    ops[pl.ds(rel, rows), from_source(last)], blocks[c, from_source(last), lane],
+                    ops[pl.ds(rel, rows), from_source(final)], blocks[c, from_source(final), lane],
                     preferred_element_type=jnp.float32)
                 res[d, c, :, lane] = total.astype(res.dtype)
-                for mask in reversed(range(1 if d == 0 else 0, g)):
-                    to = flip(mask)
+                for mask in range(1 if d == 0 else 0, g):
+                    to = flip(mask) if d == 0 else mask
                     remote(res.at[d, c, pl.ds(pl.multiple_of(to * outrows, outrows), outrows), lane],
-                           out_ref.at[c, :, target], res_send.at[d], out_recv, to, near(d)).start()
+                           out_ref.at[c, :, target], res_send.at[d, i], arrival, to, near(d)).start()
                 if d == 0:
                     pltpu.make_async_copy(
                         res.at[d, c, pl.ds(pl.multiple_of(j * outrows, outrows), outrows), lane],
-                        out_ref.at[c, :, target], out_recv).start()
+                        out_ref.at[c, :, target], arrival).start()
             return carry
 
-        lax.fori_loop(0, chunks, one, 0)
+        lax.fori_loop(0, raw, one, 0)
         wait_bytes(op_part(0, 0), op_send.at[0])
-        wait_bytes(blocks.at[:, from_source(0), :], own_send)
-        for d in range(1, half):
-            wait_bytes(blocks.at[:, from_source(0), :], fwd_send.at[d - 1])
+        for i in range(raw):
+            wait_bytes(block_part(0, i), own_send.at[i])
+            for d in range(1, half):
+                wait_bytes(block_part(0, i), fwd_send.at[d - 1, i])
+            for d in range(half):
+                sent = rows - outrows if d == 0 else rows
+                wait_bytes(res.at[d, 0, pl.ds(0, sent), pl.ds(0, width)], res_send.at[d, i])
         for s in sources:
             wait_bytes(ops.at[pl.ds(0, (g - 1) * piece), from_source(0)], spread_send.at[s])
-        for d in range(half):
-            sent = rows - outrows if d == 0 else rows
-            wait_bytes(res.at[d, :, pl.ds(0, sent), :], res_send.at[d])
+        wait_bytes(far_terms, far_send)
+        wait_bytes(near_terms.at[pl.ds(0, half * rows - outrows), :], near_send)
 
     @pl.when(jnp.logical_not(is_centre))
     def _():
         op_out(1, side, centre)
-        block_out(0, centre)
+        far_op.start()
+        tail_in.start()
         pl.semaphore_wait(ready.at[rounds], 1)
         op_out(0, 1 - side, other)
-        for i in range(1, chunks):
+        for i in range(chunks):
             block_out(i, centre)
         plane_entered()
         signal(ready.at[rounds], j, centre)
+        own_part()
+        away = step * (centre - k) - 1
+        for at, (d, to) in enumerate(owners):
+            band = far_rows(d, to)
+            remote(part.at[band, :], part_in.at[away, band, :], part_send, part_recv.at[away, at], j, centre).start()
         wait_bytes(op_part(0, 0), op_send.at[0])
         wait_bytes(op_part(0, 0), op_send.at[1])
-        wait_bytes(blocks.at[:, from_source(0), :], own_send)
-
-    wait_bytes(out_ref, out_recv)
+        for i in range(chunks):
+            wait_bytes(block_part(0, i), own_send.at[i])
+        wait_bytes(part, part_send)
+
+    for half_of in range(2):
+        wait_bytes(terms.at[half_of], terms_recv.at[half_of])
+    last[...] = (terms[0].astype(jnp.float32) + terms[1].astype(jnp.float32)).astype(last.dtype)
+    for s in range(g):
+        pltpu.make_async_copy(
+            last.at[:, pl.ds(s * width, width)],
+            out_ref.at[planes - 1, :, pl.ds(s * cols + (parts - 1) * width, width)], last_copy).start()
+    wait_bytes(out_ref.at[pl.ds(0, planes - 1)], out_recv.at[0])
+    if parts > 1:
+        wait_bytes(out_ref.at[planes - 1, :, pl.ds(0, g * width * (parts - 1))], out_recv.at[1])
+    wait_bytes(last, last_copy)
 
 
 def at_centres(n, g, products, operator):
@@ -220,6 +311,7 @@
     parts = 2 if cols % (2 * LANES) == 0 else 1
     half = n // 2
     chunks = planes * parts
+    width, outer = cols // parts, max(half - 1, 1)
     out = pl.pallas_call(
         functools.partial(kernel, n, g, parts),
         out_shape=jax.ShapeDtypeStruct((planes, rows // g, cols * g), jnp.bfloat16),
@@ -229,17 +321,31 @@
             pltpu.VMEM((planes, n * rows, cols), jnp.bfloat16),
             pltpu.VMEM((half * rows, n * rows), jnp.bfloat16),
             pltpu.VMEM((half, planes, rows, cols), jnp.bfloat16),
-            pltpu.SemaphoreType.DMA,
-            pltpu.SemaphoreType.DMA((half,)),
+            pltpu.SemaphoreType.DMA((chunks,)),
+            pltpu.SemaphoreType.DMA((half, chunks)),
             pltpu.SemaphoreType.DMA((2,)),
             pltpu.SemaphoreType.DMA((n,)),
-            pltpu.SemaphoreType.DMA((half,)),
+            pltpu.SemaphoreType.DMA((half, chunks)),
             pltpu.SemaphoreType.DMA((n, chunks)),
             pltpu.SemaphoreType.DMA((n, g)),
+            pltpu.SemaphoreType.DMA((2,)),
+            pltpu.SemaphoreType.DMA((4,)),
+            pltpu.SemaphoreType.REGULAR((g.bit_length() + 1,)),
+            pltpu.VMEM((half * rows, width), jnp.float32),
+            pltpu.VMEM((half * rows, rows), jnp.bfloat16),
+            pltpu.VMEM((rows, width), jnp.bfloat16),
+            pltpu.VMEM((half * rows, width), jnp.float32),
+            pltpu.VMEM((outer, half * rows, width), jnp.float32),
+            pltpu.VMEM((half * rows, width), jnp.bfloat16),
+            pltpu.VMEM((half * rows, width), jnp.bfloat16),
+            pltpu.VMEM((2, rows // g, g * width), jnp.bfloat16),
+            pltpu.VMEM((rows // g, g * width), jnp.bfloat16),
+            pltpu.SemaphoreType.DMA,
+            pltpu.SemaphoreType.DMA((outer, half * g)),
+            pltpu.SemaphoreType.DMA,
             pltpu.SemaphoreType.DMA,
             pltpu.SemaphoreType.DMA((2,)),
-            pltpu.SemaphoreType.REGULAR((g.bit_length(),)),
-            pltpu.VMEM((half * rows, cols // parts), jnp.float32),
+            pltpu.SemaphoreType.DMA,
         ],
         compiler_params=pltpu.CompilerParams(
             collective_id=0, has_side_effects=True, vmem_limit_bytes=GRANT),

time: 40.8 us -> 40.2 us (0.985)
  Pallas kernels: 39.9 us -> 39.2 us
    pallas_call x1, Pallas kernels: 39.9 us -> 39.2 us  [at_centres(): pl.pallas_call(functools.partial(kernel, n, g, parts), out_shape=jax.Shap...]
where the time goes in v1:
time: 40.2 us; the launch traced here: 40.1 us
  Pallas kernels  39.2 us (98%)
  local copies, waits for them, and re-layouts  0.82 us (2%)
    pallas_call x1, Pallas kernels, at_centres(): pl.pallas_call(functools.partial(kernel, n, g, parts), out_shape=jax.Shap...  39.2 us
    unnamed x1, local copies, waits for them, and re-layouts  0.82 us

profile of v1, /device:TPU:0, one launch (start us, length us, event | category | flops | bytes accessed | tf_op | source)
XLA Modules:
  0.0 40.1 jit_solution(8883893643194848633)
XLA Ops:
  0.0 39.2 %shard_map.28 = bf16[3,48,2048]{2,1,0:T(8,128)(2,1)S(1)} custom-call(bf16[3,384,256]{2,1,0:T(8,128)(2,1)} %bitcast.3, bf16[1536,384]{1,0:T(8,128)(2,1)} %op_ref.1), custom_call_target="tpu_custom_call" | custom-call | tf_op jit(solution)/shard_map/pallas_call | solution.py:315
  39.2 0.8 %copy.4 = bf16[48,3,2048]{2,0,1:T(8,128)(2,1)} copy(bf16[48,3,2048]{2,0,1:T(8,128)(2,1)S(1)} %bitcast.2) | data formatting | bytes 1179648

commit v2 on v0

v2 whole, which is shorter than its diff:
```python
import functools

import jax
import jax.numpy as jnp
from jax import lax
from jax.experimental import pallas as pl
from jax.experimental.pallas import tpu as pltpu
from jax.sharding import PartitionSpec as P

MESH = pl.DeviceIdType.MESH
LANES = 128
SUBLANES = 16
VMEM_BYTES = 60 * 1024 * 1024
GRANT = 54500 * 1024


def kernel(n, g, parts, p_ref, op_ref, out_ref, blocks, ops, far_ops, passing, res, wide, part, part_out, part_in,
           far_out, far_in, near_sum, late, own_send, fwd_send, op_send, spread_send, res_send, part_send, far_send,
           late_send, blk_recv, op_recv, pass_recv, plane_recv, sibling_recv, out_recv, part_recv, far_recv, own_copy,
           ready):
    j, k = lax.axis_index("gx"), lax.axis_index("gy")
    half = n // 2
    side = lax.div(k, half)
    step = 1 - 2 * side
    centre = jnp.where(side == 0, half - 1, half)
    other = n - 1 - centre
    is_centre = k == centre
    away = step * (centre - k)
    planes, rows, cols = p_ref.shape
    width = cols // parts
    raw = (planes - 1) * parts
    outrows = rows // g
    mine = pl.ds(pl.multiple_of(side * (half * rows), half * rows), half * rows)
    theirs = pl.ds(pl.multiple_of((1 - side) * (half * rows), half * rows), half * rows)

    def flip(mask):
        to = j
        for bit in (1 << b for b in range(mask.bit_length())):
            if mask & bit:
                to = to + bit * (1 - 2 * lax.rem(lax.div(j, bit), 2))
        return to

    def near(d):
        return centre - step * d

    def far(d):
        return other + step * d

    def from_source(s):
        return pl.ds(pl.multiple_of(s * rows, rows), rows)

    def near_rows(d, to, count=1):
        at = (near(d) - side * half) * rows + to * outrows
        return pl.ds(pl.multiple_of(at, outrows), count * outrows)

    def far_rows(d, to, count=1):
        at = (far(d) - (1 - side) * half) * rows + to * outrows
        return pl.ds(pl.multiple_of(at, outrows), count * outrows)

    def wait_bytes(ref, sem):
        pltpu.make_async_copy(ref, ref, sem).wait()

    def op_bytes(pieces):
        return ops.at[pl.ds(0, pieces * outrows), pl.ds(0, rows)]

    own_far = pltpu.make_async_copy(op_ref.at[theirs, :], far_ops, own_copy.at[0])
    own_far.start()
    own_blocks = pltpu.make_async_copy(p_ref, blocks.at[:, from_source(k), :], own_copy.at[1])
    own_blocks.start()
    own_ops = pltpu.make_async_copy(op_ref.at[mine, :], ops.at[:, from_source(k)], own_copy.at[2])
    own_ops.start()

    rounds = g.bit_length() - 1
    barrier = pltpu.get_barrier_semaphore()

    def signal(sem, gx, gy):
        pl.semaphore_signal(sem, inc=1, device_id=(gx, gy), device_id_type=MESH)

    for b in range(rounds):
        signal(barrier, flip(1 << b), k)

    @pl.when(is_centre)
    def _():
        signal(barrier, j, other)
        for d in range(1, half):
            signal(barrier, j, near(d))

    pl.semaphore_wait(barrier, rounds + 1)

    def plane_entered():
        for b in range(rounds):
            signal(ready.at[b], flip(1 << b), k)
            pl.semaphore_wait(ready.at[b], 1)

    def remote(src, dst, send, recv, gx, gy):
        return pltpu.make_async_remote_copy(
            src_ref=src, dst_ref=dst, send_sem=send, recv_sem=recv,
            device_id=(gx, gy), device_id_type=MESH)

    def lanes(i):
        return pl.ds(pl.multiple_of(lax.rem(i, parts) * width, width), width)

    def block_part(s, i):
        return blocks.at[lax.div(i, parts), from_source(s), lanes(i)]

    def last_plane(s):
        return blocks.at[planes - 1, from_source(s), :]

    sources = [near(d) for d in range(1, half)] + [far(d) for d in range(half)]

    def hops(owner):
        d, chip = owner
        return bin(chip).count("1") - d, chip

    pairs = sorted(((d, chip) for d in range(half) for chip in range(g // 2)), key=hops)
    outer_first = list(reversed(range(half)))

    def own_part():
        part[...] = jnp.dot(far_ops[...], last_plane(k)[...], preferred_element_type=jnp.float32)

    @pl.when(is_centre)
    def _():
        def block_out(i):
            at = block_part(k, i)
            remote(at, at, own_send, blk_recv.at[half - 1, i], j, other).start()

        own_far.wait()
        for d in outer_first:
            remote(far_ops.at[far_rows(d, j), :], ops.at[far_rows(d, j), from_source(k)],
                   op_send, op_recv.at[half - 1, d], j, other).start()
        own_blocks.wait()
        block_out(0)
        block_out(1)
        own_part()

        def spread(e, d, at, mask):
            part_of = ops.at[near_rows(d, at), from_source(sources[e])]
            sem = sibling_recv.at[d] if mask == 1 else plane_recv.at[e, d]
            remote(part_of, part_of, spread_send.at[e], sem, flip(mask), k).start()

        adjacent = [1 << b for b in reversed(range(rounds))]
        distant = [2 * m for m in range(1, g // 2) if 2 * m not in adjacent]

        def enter(e, d):
            wait_bytes(op_bytes(1), op_recv.at[e, d])
            for mask in adjacent:
                spread(e, d, j, mask)

        def enter_distant(e, d):
            for mask in distant:
                spread(e, d, j, mask)

        def share(d):
            for e in range(len(sources)):
                wait_bytes(op_bytes(g // 2 - 1), plane_recv.at[e, d])
                for mask in range(1, g // 2):
                    spread(e, d, flip(2 * mask), 1)

        def complete(d):
            wait_bytes(op_bytes(len(sources) * (g // 2)), sibling_recv.at[d])

        def pass_on(d):
            for m in range(half - 1):
                wait_bytes(op_bytes(1), pass_recv.at[m, d])
                remote(passing.at[m, d], ops.at[far_rows(d, j), from_source(near(m + 1))],
                       op_send, op_recv.at[half + m, d], j, other).start()

        def forward(i):
            for m in range(half - 1):
                at = block_part(near(m + 1), i)
                wait_bytes(at, blk_recv.at[m, i])
                remote(at, at, fwd_send.at[m], blk_recv.at[half + m, i], j, other).start()

        closest, rest = range(half), range(half, 2 * half - 1)
        first = half - 1
        for e in closest[:1]:
            enter(e, first)
        plane_entered()
        for e in closest[:1]:
            enter_distant(e, first)
        for e in closest[1:]:
            enter(e, first)
            enter_distant(e, first)
        for d in outer_first:
            pass_on(d)
        block_out(2)
        for e in rest:
            enter(e, first)
            enter_distant(e, first)
        for d in outer_first[1:]:
            for e in range(len(sources)):
                enter(e, d)
                enter_distant(e, d)
        forward(0)
        forward(1)
        own_ops.wait()
        share(first)
        complete(first)
        if half > 1:
            pl.semaphore_wait(ready.at[rounds], half - 1)
        forward(2)
        for i in range(3, raw):
            block_out(i)

        band_of = lambda d: from_source(near(d) - side * half)
        others = pl.ds(pl.multiple_of(side * rows, rows), (n - 1) * rows)
        final = far(half - 1)

        def results(d, c, lane, size):
            target = pl.ds(pl.multiple_of(j * cols + lane, width), size)
            lane = pl.ds(lane, size)

            def result(to):
                return res.at[d, c, pl.ds(pl.multiple_of(to * outrows, outrows), outrows), lane]

            @pl.when(d > 0)
            def _():
                for to in range(g):
                    remote(result(to), out_ref.at[c, :, target], res_send.at[d], out_recv.at[0], to, near(d)).start()

            @pl.when(d == 0)
            def _():
                for mask in range(1, g):
                    to = flip(mask)
                    remote(result(to), out_ref.at[c, :, target], res_send.at[d], out_recv.at[0], to, near(d)).start()
                pltpu.make_async_copy(result(j), out_ref.at[c, :, target], out_recv.at[0]).start()

        def product(d, c, lane, i_first, count):
            band = band_of(d)

            @pl.when(d == first)
            def _():
                for e in range(half - 1):
                    for i in range(count):
                        wait_bytes(block_part(0, 0), blk_recv.at[half - 1 + e, i_first + i])
            size = lane.size
            ahead = wide.at[:, pl.ds(0, size)]
            ahead[...] = jnp.dot(ops[band, others], blocks[c, others, lane], preferred_element_type=jnp.float32)

            @pl.when(d == first)
            def _():
                for i in range(count):
                    wait_bytes(block_part(0, 0), blk_recv.at[2 * half - 2, i_first + i])
            total = ahead[...] + jnp.dot(
                ops[band, from_source(final)], blocks[c, from_source(final), lane], preferred_element_type=jnp.float32)
            res[d, c, :, lane] = total.astype(res.dtype)

        def near_half():
            for m in range(half - 1):
                wait_bytes(last_plane(0), blk_recv.at[m, raw])
            near_sum[...] = jnp.dot(ops[:, mine], blocks[planes - 1, mine, :], preferred_element_type=jnp.float32)

        def far_half(at):
            d, chip = pairs[at]
            band = far_rows(d, 2 * chip, 2)
            total = part[band, :]
            for m in range(half - 1):
                wait_bytes(part_in.at[m, band, :], part_recv.at[m, at])
                total = total + part_in[m, band, :].astype(jnp.float32)
            far_out[band, :] = total.astype(far_out.dtype)
            remote(far_out.at[band, :], far_in.at[band, :], far_send, far_recv.at[at], j, other).start()

        def late_result(at):
            d, chip = pairs[at]
            band = near_rows(d, 2 * chip, 2)
            wait_bytes(far_in.at[band, :], far_recv.at[at])
            late[band, :] = (near_sum[band, :] + far_in[band, :].astype(jnp.float32)).astype(late.dtype)
            target = out_ref.at[planes - 1, :, pl.ds(pl.multiple_of(j * cols, cols), cols)]
            for to in (2 * chip, 2 * chip + 1):
                def send(to=to):
                    remote(late.at[near_rows(d, to), :], target, late_send, out_recv.at[1], to, near(d)).start()

                if d > 0:
                    send()
                else:
                    pl.when(j != to)(send)

                    @pl.when(j == to)
                    def _(to=to):
                        pltpu.make_async_copy(late.at[near_rows(d, to), :], target, out_recv.at[1]).start()

        def whole_plane(t, carry):
            c, d = lax.div(t, half), first - lax.rem(t, half)

            @pl.when(t == 1)
            def _():
                for e in outer_first[1:]:
                    share(e)
                    complete(e)
            product(d, c, pl.ds(0, cols), c * parts, parts)
            results(d, c, 0, cols)

            @pl.when(t == 0)
            def _():
                for i in range(3, raw):
                    forward(i)
            return carry

        def one_chunk(t, carry):
            h, d = lax.div(t, half), first - lax.rem(t, half)
            at = pl.multiple_of(h * width, width)

            @pl.when(t == half * (parts - 1))
            def _():
                for e in range(len(pairs) // 2):
                    far_half(e)
            i = (planes - 2) * parts + h
            product(d, planes - 2, pl.ds(at, width), i, 1)
            results(d, planes - 2, at, width)
            return carry

        lax.fori_loop(0, half * (planes - 2), whole_plane, 0)
        lax.fori_loop(0, half * parts, one_chunk, 0)
        near_half()
        split = len(pairs) // 2
        for at in range(split, len(pairs)):
            far_half(at)
            late_result(at - split)
        for at in range(len(pairs) - split, len(pairs)):
            late_result(at)
        wait_bytes(op_bytes(half * half), op_send)
        wait_bytes(blocks.at[pl.ds(0, planes - 1), from_source(0), :], own_send)
        for m in range(half - 1):
            wait_bytes(blocks.at[pl.ds(0, planes - 1), from_source(0), :], fwd_send.at[m])
        for d in range(half):
            sent = rows - outrows if d == 0 else rows
            wait_bytes(res.at[d, pl.ds(0, planes - 1), pl.ds(0, sent), :], res_send.at[d])
        for e in range(len(sources)):
            wait_bytes(op_bytes(half * (g - 1)), spread_send.at[e])
        wait_bytes(far_out, far_send)
        wait_bytes(late.at[pl.ds(0, half * rows - outrows), :], late_send)

    @pl.when(jnp.logical_not(is_centre))
    def _():
        m = away - 1

        def op_in(d):
            at = ops.at[near_rows(d, j), from_source(k)]
            remote(at, at, op_send, op_recv.at[m, d], j, centre).start()

        def op_past(d):
            remote(far_ops.at[far_rows(d, j), :], passing.at[m, d], op_send, pass_recv.at[m, d], j, centre).start()

        own_ops.wait()
        op_in(half - 1)
        own_far.wait()
        for d in outer_first:
            op_past(d)
        for d in outer_first[1:]:
            op_in(d)
        own_blocks.wait()
        for i in range(raw):
            at = block_part(k, i)
            remote(at, at, own_send, blk_recv.at[m, i], j, centre).start()
        own_part()
        part_out[...] = part[...].astype(part_out.dtype)
        for at, (d, chip) in enumerate(pairs):
            if at == len(pairs) // 2:
                remote(last_plane(k), last_plane(k), own_send, blk_recv.at[m, raw], j, centre).start()
            band = far_rows(d, 2 * chip, 2)
            remote(part_out.at[band, :], part_in.at[m, band, :], part_send, part_recv.at[m, at], j, centre).start()
        plane_entered()
        signal(ready.at[rounds], j, centre)
        wait_bytes(op_bytes(2 * half), op_send)
        wait_bytes(blocks.at[:, from_source(0), :], own_send)
        wait_bytes(part_out, part_send)

    wait_bytes(out_ref.at[pl.ds(0, planes - 1)], out_recv.at[0])
    wait_bytes(out_ref.at[planes - 1], out_recv.at[1])


def at_centres(n, g, products, operator):
    rows, planes, cols = products.shape
    parts = 2 if cols % (2 * LANES) == 0 else 1
    half = n // 2
    outer, roles, raw = max(half - 1, 1), 2 * half - 1, (planes - 1) * parts
    out = pl.pallas_call(
        functools.partial(kernel, n, g, parts),
        out_shape=jax.ShapeDtypeStruct((planes, rows // g, cols * g), jnp.bfloat16),
        in_specs=[pl.BlockSpec(memory_space=pl.ANY)] * 2,
        out_specs=pl.BlockSpec(memory_space=pl.ANY),
        scratch_shapes=[
            pltpu.VMEM((planes, n * rows, cols), jnp.bfloat16),
            pltpu.VMEM((half * rows, n * rows), jnp.bfloat16),
            pltpu.VMEM((half * rows, rows), jnp.bfloat16),
            pltpu.VMEM((outer, half, rows // g, rows), jnp.bfloat16),
            pltpu.VMEM((half, planes - 1, rows, cols), jnp.bfloat16),
            pltpu.VMEM((rows, cols), jnp.float32),
            pltpu.VMEM((half * rows, cols), jnp.float32),
            pltpu.VMEM((half * rows, cols), jnp.bfloat16),
            pltpu.VMEM((outer, half * rows, cols), jnp.bfloat16),
            pltpu.VMEM((half * rows, cols), jnp.bfloat16),
            pltpu.VMEM((half * rows, cols), jnp.bfloat16),
            pltpu.VMEM((half * rows, cols), jnp.float32),
            pltpu.VMEM((half * rows, cols), jnp.bfloat16),
            pltpu.SemaphoreType.DMA,
            pltpu.SemaphoreType.DMA((outer,)),
            pltpu.SemaphoreType.DMA,
            pltpu.SemaphoreType.DMA((roles,)),
            pltpu.SemaphoreType.DMA((half,)),
            pltpu.SemaphoreType.DMA,
            pltpu.SemaphoreType.DMA,
            pltpu.SemaphoreType.DMA,
            pltpu.SemaphoreType.DMA((roles, raw + 1)),
            pltpu.SemaphoreType.DMA((roles, half)),
            pltpu.SemaphoreType.DMA((outer, half)),
            pltpu.SemaphoreType.DMA((roles, half)),
            pltpu.SemaphoreType.DMA((half,)),
            pltpu.SemaphoreType.DMA((2,)),
            pltpu.SemaphoreType.DMA((outer, half * g // 2)),
            pltpu.SemaphoreType.DMA((half * g // 2,)),
            pltpu.SemaphoreType.DMA((3,)),
            pltpu.SemaphoreType.REGULAR((g.bit_length(),)),
        ],
        compiler_params=pltpu.CompilerParams(
            collective_id=0, has_side_effects=True, vmem_limit_bytes=GRANT),
    )(products.transpose(1, 0, 2), operator)
    return out.transpose(1, 0, 2)


def by_collectives(products, operator):
    y_local, three, m_local = products.shape
    flat = products.reshape(y_local, three * m_local)
    summed = lax.psum_scatter(
        jnp.dot(operator, flat, preferred_element_type=jnp.float32), "gy", scatter_dimension=0, tiled=True)
    result = summed.astype(jnp.bfloat16).reshape(y_local, three, m_local)
    return lax.all_to_all(result, "gx", split_axis=0, concat_axis=2, tiled=True)


def solution(mesh):
    n, g = mesh.shape["gy"], mesh.shape["gx"]

    def body(products, operator):
        rows, planes, cols = products.shape
        aligned = (n % 2 == 0 and n > 2 and planes > 2 and g & (g - 1) == 0 and g > 1 and rows % (g * SUBLANES) == 0
                   and rows % LANES == 0 and cols % LANES == 0)
        held = 2 * (products.size * (n + n // 2 + 2) + operator.size * (2 + n // 2)) + 20 * n * rows * cols
        if aligned and held < VMEM_BYTES // 2:
            return at_centres(n, g, products, operator)
        return by_collectives(products, operator)

    return jax.shard_map(
        body,
        mesh=mesh,
        in_specs=(P("gy", None, "gx"), P(None, "gy")),
        out_specs=P(("gy", "gx"), None, None),
        check_vma=False,
    )
```

time: 40.8 us -> 38.2 us (0.936)
  the two profiles are of different devices: /device:TPU:0 before, /device:TPU:7 now
where the time goes in v2:
time: 38.2 us; the launch traced here: 38 us
  Pallas kernels  37.2 us (97%)
  local copies, waits for them, and re-layouts  0.82 us (2%)
    pallas_call x1, Pallas kernels, at_centres(): pl.pallas_call(functools.partial(kernel, n, g, parts), out_shape=jax.Shap...  37.2 us
    unnamed x1, local copies, waits for them, and re-layouts  0.82 us

profile of v2, /device:TPU:7, one launch (start us, length us, event | category | flops | bytes accessed | tf_op | source)
XLA Modules:
  0.0 38.0 jit_solution(2895099553796982916)
XLA Ops:
  0.0 37.2 %shard_map.28 = bf16[3,48,2048]{2,1,0:T(8,128)(2,1)S(1)} custom-call(bf16[3,384,256]{2,1,0:T(8,128)(2,1)} %bitcast.3, bf16[1536,384]{1,0:T(8,128)(2,1)} %op_ref.1), custom_call_target="tpu_custom_call" | custom-call | tf_op jit(solution)/shard_map/pallas_call | solution.py:377
  37.2 0.8 %copy.4 = bf16[48,3,2048]{2,0,1:T(8,128)(2,1)} copy(bf16[48,3,2048]{2,0,1:T(8,128)(2,1)S(1)} %bitcast.2) | data formatting | bytes 1179648

commit v3 on v2

--- a/solution.py
+++ b/solution.py
@@ -14,9 +14,9 @@
 GRANT = 54500 * 1024
 
 
-def kernel(n, g, parts, p_ref, op_ref, out_ref, blocks, ops, far_ops, passing, res, wide, part, part_out, part_in,
-           far_out, far_in, near_sum, late, own_send, fwd_send, op_send, spread_send, res_send, part_send, far_send,
-           late_send, blk_recv, op_recv, pass_recv, plane_recv, sibling_recv, out_recv, part_recv, far_recv, own_copy,
+def kernel(n, g, parts, p_ref, op_ref, out_ref, blocks, ops, far_ops, first_ops, passing, res, wide, part, part_out, part_in,
+           far_out, far_in, near_sum, near_out, late, terms, last, own_send, fwd_send, op_send, spread_send, res_send, part_send, far_send,
+           late_send, near_send, blk_recv, op_recv, pass_recv, plane_recv, sibling_recv, out_recv, part_recv, far_recv, terms_recv, own_copy,
            ready):
     j, k = lax.axis_index("gx"), lax.axis_index("gy")
     half = n // 2
@@ -63,12 +63,28 @@
     def op_bytes(pieces):
         return ops.at[pl.ds(0, pieces * outrows), pl.ds(0, rows)]
 
-    own_far = pltpu.make_async_copy(op_ref.at[theirs, :], far_ops, own_copy.at[0])
-    own_far.start()
-    own_blocks = pltpu.make_async_copy(p_ref, blocks.at[:, from_source(k), :], own_copy.at[1])
-    own_blocks.start()
-    own_ops = pltpu.make_async_copy(op_ref.at[mine, :], ops.at[:, from_source(k)], own_copy.at[2])
-    own_ops.start()
+    def staged(slot, d):
+        at = far_rows(d, j) if slot == 0 else near_rows(d, j)
+        start = (theirs if slot == 0 else mine).start
+        return pltpu.make_async_copy(
+            op_ref.at[pl.ds(pl.multiple_of(start + at.start, outrows), outrows), :], first_ops.at[slot, d],
+            own_copy.at[2 * d + slot])
+
+    own_start = pltpu.make_async_copy(
+        p_ref.at[0, :, pl.ds(0, width)], blocks.at[0, from_source(k), pl.ds(0, width)], own_copy.at[2 * half])
+    own_rest = [pltpu.make_async_copy(
+        p_ref.at[0, :, pl.ds(width, cols - width)], blocks.at[0, from_source(k), pl.ds(width, cols - width)],
+        own_copy.at[2 * half + 1])] if parts > 1 else []
+    own_rest.append(pltpu.make_async_copy(
+        p_ref.at[pl.ds(1, planes - 1)], blocks.at[pl.ds(1, planes - 1), from_source(k), :], own_copy.at[2 * half + 2]))
+    own_far = pltpu.make_async_copy(op_ref.at[theirs, :], far_ops, own_copy.at[2 * half + 3])
+    own_ops = pltpu.make_async_copy(op_ref.at[mine, :], ops.at[:, from_source(k)], own_copy.at[2 * half + 4])
+    for d in reversed(range(half)):
+        for slot in (1, 0):
+            staged(slot, d).start()
+    own_start.start()
+    for rest_of in own_rest + [own_far, own_ops]:
+        rest_of.start()
 
     rounds = g.bit_length() - 1
     barrier = pltpu.get_barrier_semaphore()
@@ -108,12 +124,22 @@
 
     sources = [near(d) for d in range(1, half)] + [far(d) for d in range(half)]
 
-    def hops(owner):
-        d, chip = owner
-        return bin(chip).count("1") - d, chip
-
-    pairs = sorted(((d, chip) for d in range(half) for chip in range(g // 2)), key=hops)
+    chips = g // 2
+    column = lax.div(j, 2)
+
+    def pick(at):
+        chip = jnp.int32(0)
+        for c in range(chips):
+            order = sorted(range(1, chips), key=lambda x: (-bin(x ^ c).count("1"), x))
+            chip = jnp.where(column == c, order[at], chip)
+        return chip
+
+    held_back = half * chips * 3 // 4
+    turns = [pick(at) for at in range(chips - 1)]
     outer_first = list(reversed(range(half)))
+    pairs = [(d, 0) for d in outer_first[:-1]] + [(d, chip) for d in outer_first[:-1] for chip in turns]
+    joined = len(pairs)
+    pairs += [(0, chip) for chip in [0] + turns]
 
     def own_part():
         part[...] = jnp.dot(far_ops[...], last_plane(k)[...], preferred_element_type=jnp.float32)
@@ -124,13 +150,18 @@
             at = block_part(k, i)
             remote(at, at, own_send, blk_recv.at[half - 1, i], j, other).start()
 
+        for d in outer_first:
+            staged(0, d).wait()
+            remote(first_ops.at[0, d], ops.at[far_rows(d, j), from_source(k)],
+                   op_send, op_recv.at[half - 1, d], j, other).start()
+        own_start.wait()
+        block_out(0)
+        for rest_of in own_rest:
+            rest_of.wait()
+        block_out(1)
+        for d in outer_first:
+            staged(1, d).wait()
         own_far.wait()
-        for d in outer_first:
-            remote(far_ops.at[far_rows(d, j), :], ops.at[far_rows(d, j), from_source(k)],
-                   op_send, op_recv.at[half - 1, d], j, other).start()
-        own_blocks.wait()
-        block_out(0)
-        block_out(1)
         own_part()
 
         def spread(e, d, at, mask):
@@ -176,6 +207,7 @@
         for e in closest[:1]:
             enter(e, first)
         plane_entered()
+        signal(ready.at[rounds + 1], j, other)
         for e in closest[:1]:
             enter_distant(e, first)
         for e in closest[1:]:
@@ -249,6 +281,14 @@
             for m in range(half - 1):
                 wait_bytes(last_plane(0), blk_recv.at[m, raw])
             near_sum[...] = jnp.dot(ops[:, mine], blocks[planes - 1, mine, :], preferred_element_type=jnp.float32)
+            near_out[...] = near_sum[band_of(0), :].astype(near_out.dtype)
+            target = terms.at[1, :, pl.ds(pl.multiple_of(j * cols, cols), cols)]
+
+            def term(to):
+                return near_out.at[pl.ds(pl.multiple_of(to * outrows, outrows), outrows), :]
+            for mask in reversed(range(1, g)):
+                remote(term(flip(mask)), target, near_send, terms_recv.at[1], flip(mask), k).start()
+            pltpu.make_async_copy(term(j), target, terms_recv.at[1]).start()
 
         def far_half(at):
             d, chip = pairs[at]
@@ -258,7 +298,12 @@
                 wait_bytes(part_in.at[m, band, :], part_recv.at[m, at])
                 total = total + part_in[m, band, :].astype(jnp.float32)
             far_out[band, :] = total.astype(far_out.dtype)
-            remote(far_out.at[band, :], far_in.at[band, :], far_send, far_recv.at[at], j, other).start()
+            if at < joined:
+                remote(far_out.at[band, :], far_in.at[band, :], far_send, far_recv.at[at], j, other).start()
+                return
+            for to in (2 * chip, 2 * chip + 1):
+                remote(far_out.at[far_rows(d, to), :], terms.at[0, :, pl.ds(pl.multiple_of(j * cols, cols), cols)],
+                       far_send, terms_recv.at[0], to, other).start()
 
         def late_result(at):
             d, chip = pairs[at]
@@ -267,17 +312,7 @@
             late[band, :] = (near_sum[band, :] + far_in[band, :].astype(jnp.float32)).astype(late.dtype)
             target = out_ref.at[planes - 1, :, pl.ds(pl.multiple_of(j * cols, cols), cols)]
             for to in (2 * chip, 2 * chip + 1):
-                def send(to=to):
-                    remote(late.at[near_rows(d, to), :], target, late_send, out_recv.at[1], to, near(d)).start()
-
-                if d > 0:
-                    send()
-                else:
-                    pl.when(j != to)(send)
-
-                    @pl.when(j == to)
-                    def _(to=to):
-                        pltpu.make_async_copy(late.at[near_rows(d, to), :], target, out_recv.at[1]).start()
+                remote(late.at[near_rows(d, to), :], target, late_send, out_recv.at[1], to, near(d)).start()
 
         def whole_plane(t, carry):
             c, d = lax.div(t, half), first - lax.rem(t, half)
@@ -300,9 +335,14 @@
             h, d = lax.div(t, half), first - lax.rem(t, half)
             at = pl.multiple_of(h * width, width)
 
+            @pl.when(t == max(half * (parts - 1) - 1, 0))
+            def _():
+                for e in range(len(pairs) // 4):
+                    far_half(e)
+
             @pl.when(t == half * (parts - 1))
             def _():
-                for e in range(len(pairs) // 2):
+                for e in range(len(pairs) // 4, len(pairs) // 2):
                     far_half(e)
             i = (planes - 2) * parts + h
             product(d, planes - 2, pl.ds(at, width), i, 1)
@@ -311,13 +351,15 @@
 
         lax.fori_loop(0, half * (planes - 2), whole_plane, 0)
         lax.fori_loop(0, half * parts, one_chunk, 0)
+        pl.semaphore_wait(ready.at[rounds + 1], 1)
+        for at in range(len(pairs) // 2, held_back):
+            far_half(at)
         near_half()
-        split = len(pairs) // 2
-        for at in range(split, len(pairs)):
-            far_half(at)
-            late_result(at - split)
-        for at in range(len(pairs) - split, len(pairs)):
-            late_result(at)
+        for at in range(max(joined, len(pairs) - held_back)):
+            if held_back + at < len(pairs):
+                far_half(held_back + at)
+            if at < joined:
+                late_result(at)
         wait_bytes(op_bytes(half * half), op_send)
         wait_bytes(blocks.at[pl.ds(0, planes - 1), from_source(0), :], own_send)
         for m in range(half - 1):
@@ -328,34 +370,42 @@
         for e in range(len(sources)):
             wait_bytes(op_bytes(half * (g - 1)), spread_send.at[e])
         wait_bytes(far_out, far_send)
-        wait_bytes(late.at[pl.ds(0, half * rows - outrows), :], late_send)
+        wait_bytes(late.at[pl.ds(0, (half - 1) * rows), :], late_send)
+        wait_bytes(near_out.at[pl.ds(0, rows - outrows), :], near_send)
+        for b in (1, 0):
+            wait_bytes(terms.at[b], terms_recv.at[b])
+        last[...] = (terms[0].astype(jnp.float32) + terms[1].astype(jnp.float32)).astype(last.dtype)
+        pltpu.make_async_copy(last, out_ref.at[planes - 1], out_recv.at[1]).start()
 
     @pl.when(jnp.logical_not(is_centre))
     def _():
         m = away - 1
 
         def op_in(d):
-            at = ops.at[near_rows(d, j), from_source(k)]
-            remote(at, at, op_send, op_recv.at[m, d], j, centre).start()
+            staged(1, d).wait()
+            remote(first_ops.at[1, d], ops.at[near_rows(d, j), from_source(k)],
+                   op_send, op_recv.at[m, d], j, centre).start()
 
         def op_past(d):
-            remote(far_ops.at[far_rows(d, j), :], passing.at[m, d], op_send, pass_recv.at[m, d], j, centre).start()
-
-        own_ops.wait()
+            staged(0, d).wait()
+            remote(first_ops.at[0, d], passing.at[m, d], op_send, pass_recv.at[m, d], j, centre).start()
+
         op_in(half - 1)
-        own_far.wait()
         for d in outer_first:
             op_past(d)
         for d in outer_first[1:]:
             op_in(d)
-        own_blocks.wait()
+        for rest_of in [own_start] + own_rest:
+            rest_of.wait()
         for i in range(raw):
             at = block_part(k, i)
             remote(at, at, own_send, blk_recv.at[m, i], j, centre).start()
+        own_far.wait()
+        own_ops.wait()
         own_part()
         part_out[...] = part[...].astype(part_out.dtype)
         for at, (d, chip) in enumerate(pairs):
-            if at == len(pairs) // 2:
+            if at == held_back:
                 remote(last_plane(k), last_plane(k), own_send, blk_recv.at[m, raw], j, centre).start()
             band = far_rows(d, 2 * chip, 2)
             remote(part_out.at[band, :], part_in.at[m, band, :], part_send, part_recv.at[m, at], j, centre).start()
@@ -383,6 +433,7 @@
             pltpu.VMEM((planes, n * rows, cols), jnp.bfloat16),
             pltpu.VMEM((half * rows, n * rows), jnp.bfloat16),
             pltpu.VMEM((half * rows, rows), jnp.bfloat16),
+            pltpu.VMEM((2, half, rows // g, rows), jnp.bfloat16),
             pltpu.VMEM((outer, half, rows // g, rows), jnp.bfloat16),
             pltpu.VMEM((half, planes - 1, rows, cols), jnp.bfloat16),
             pltpu.VMEM((rows, cols), jnp.float32),
@@ -392,12 +443,16 @@
             pltpu.VMEM((half * rows, cols), jnp.bfloat16),
             pltpu.VMEM((half * rows, cols), jnp.bfloat16),
             pltpu.VMEM((half * rows, cols), jnp.float32),
+            pltpu.VMEM((rows, cols), jnp.bfloat16),
             pltpu.VMEM((half * rows, cols), jnp.bfloat16),
+            pltpu.VMEM((2, rows // g, g * cols), jnp.bfloat16),
+            pltpu.VMEM((rows // g, g * cols), jnp.bfloat16),
             pltpu.SemaphoreType.DMA,
             pltpu.SemaphoreType.DMA((outer,)),
             pltpu.SemaphoreType.DMA,
             pltpu.SemaphoreType.DMA((roles,)),
             pltpu.SemaphoreType.DMA((half,)),
+            pltpu.SemaphoreType.DMA,
             pltpu.SemaphoreType.DMA,
             pltpu.SemaphoreType.DMA,
             pltpu.SemaphoreType.DMA,
@@ -408,9 +463,10 @@
             pltpu.SemaphoreType.DMA((half,)),
             pltpu.SemaphoreType.DMA((2,)),
             pltpu.SemaphoreType.DMA((outer, half * g // 2)),
-            pltpu.SemaphoreType.DMA((half * g // 2,)),
-            pltpu.SemaphoreType.DMA((3,)),
-            pltpu.SemaphoreType.REGULAR((g.bit_length(),)),
+            pltpu.SemaphoreType.DMA((outer * g // 2,)),
+            pltpu.SemaphoreType.DMA((2,)),
+            pltpu.SemaphoreType.DMA((2 * half + 5,)),
+            pltpu.SemaphoreType.REGULAR((g.bit_length() + 1,)),
         ],
         compiler_params=pltpu.CompilerParams(
             collective_id=0, has_side_effects=True, vmem_limit_bytes=GRANT),

time: 38.2 us -> 35.9 us (0.940)
  the two profiles are of different devices: /device:TPU:7 before, /device:TPU:5 now
where the time goes in v3:
time: 35.9 us; the launch traced here: 35.7 us
  Pallas kernels  34.9 us (97%)
  local copies, waits for them, and re-layouts  0.82 us (2%)
    pallas_call x1, Pallas kernels, at_centres(): pl.pallas_call(functools.partial(kernel, n, g, parts), out_shape=jax.Shap...  34.9 us
    unnamed x1, local copies, waits for them, and re-layouts  0.82 us

profile of v3, /device:TPU:5, one launch (start us, length us, event | category | flops | bytes accessed | tf_op | source)
XLA Modules:
  0.0 35.7 jit_solution(12057683991432631482)
XLA Ops:
  0.0 34.9 %shard_map.28 = bf16[3,48,2048]{2,1,0:T(8,128)(2,1)S(1)} custom-call(bf16[3,384,256]{2,1,0:T(8,128)(2,1)} %bitcast.3, bf16[1536,384]{1,0:T(8,128)(2,1)} %op_ref.1), custom_call_target="tpu_custom_call" | custom-call | tf_op jit(solution)/shard_map/pallas_call | solution.py:427
  34.9 0.8 %copy.4 = bf16[48,3,2048]{2,0,1:T(8,128)(2,1)} copy(bf16[48,3,2048]{2,0,1:T(8,128)(2,1)S(1)} %bitcast.2) | data formatting | bytes 1179648

commit v4 on v3

--- a/solution.py
+++ b/solution.py
@@ -127,14 +127,17 @@
     chips = g // 2
     column = lax.div(j, 2)
 
+    def bits(x):
+        return bin(x).count("1")
+
     def pick(at):
         chip = jnp.int32(0)
         for c in range(chips):
-            order = sorted(range(1, chips), key=lambda x: (-bin(x ^ c).count("1"), x))
+            order = sorted(range(1, chips), key=lambda x: (bits(x) - bits(x ^ c), x == c, x))
             chip = jnp.where(column == c, order[at], chip)
         return chip
 
-    held_back = half * chips * 3 // 4
+    held_back = half * chips // 2
     turns = [pick(at) for at in range(chips - 1)]
     outer_first = list(reversed(range(half)))
     pairs = [(d, 0) for d in outer_first[:-1]] + [(d, chip) for d in outer_first[:-1] for chip in turns]
@@ -172,13 +175,9 @@
         adjacent = [1 << b for b in reversed(range(rounds))]
         distant = [2 * m for m in range(1, g // 2) if 2 * m not in adjacent]
 
-        def enter(e, d):
+        def enter(e, d, everywhere):
             wait_bytes(op_bytes(1), op_recv.at[e, d])
-            for mask in adjacent:
-                spread(e, d, j, mask)
-
-        def enter_distant(e, d):
-            for mask in distant:
+            for mask in (distant if everywhere else []) + adjacent:
                 spread(e, d, j, mask)
 
         def share(d):
@@ -204,35 +203,31 @@
 
         closest, rest = range(half), range(half, 2 * half - 1)
         first = half - 1
-        for e in closest[:1]:
-            enter(e, first)
+        enter(0, first, False)
         plane_entered()
         signal(ready.at[rounds + 1], j, other)
-        for e in closest[:1]:
-            enter_distant(e, first)
+        for mask in distant:
+            spread(0, first, j, mask)
         for e in closest[1:]:
-            enter(e, first)
-            enter_distant(e, first)
+            enter(e, first, True)
         for d in outer_first:
             pass_on(d)
         block_out(2)
+        forward(0)
         for e in rest:
-            enter(e, first)
-            enter_distant(e, first)
+            enter(e, first, True)
         for d in outer_first[1:]:
             for e in range(len(sources)):
-                enter(e, d)
-                enter_distant(e, d)
-        forward(0)
+                enter(e, d, True)
         forward(1)
         own_ops.wait()
         share(first)
+        forward(2)
+        for i in range(3, raw):
+            block_out(i)
         complete(first)
         if half > 1:
             pl.semaphore_wait(ready.at[rounds], half - 1)
-        forward(2)
-        for i in range(3, raw):
-            block_out(i)
 
         band_of = lambda d: from_source(near(d) - side * half)
         others = pl.ds(pl.multiple_of(side * rows, rows), (n - 1) * rows)
@@ -314,52 +309,59 @@
             for to in (2 * chip, 2 * chip + 1):
                 remote(late.at[near_rows(d, to), :], target, late_send, out_recv.at[1], to, near(d)).start()
 
-        def whole_plane(t, carry):
-            c, d = lax.div(t, half), first - lax.rem(t, half)
+        early = (planes - 2) * parts
+
+        def one(t, carry):
+            i = jnp.where(t < early, t, early + lax.div(t - early, half))
+            d = jnp.where(t < early, first, first - lax.rem(t - early, half))
+            c, h = lax.div(i, parts), lax.rem(i, parts)
+            at = pl.multiple_of(h * width, width)
 
             @pl.when(t == 1)
+            def _():
+                for e in range(3, raw):
+                    forward(e)
+
+            @pl.when(t == early)
             def _():
                 for e in outer_first[1:]:
                     share(e)
                     complete(e)
-            product(d, c, pl.ds(0, cols), c * parts, parts)
-            results(d, c, 0, cols)
-
-            @pl.when(t == 0)
-            def _():
-                for i in range(3, raw):
-                    forward(i)
+
+            @pl.when(t == early + 1)
+            def _():
+                near_half()
+                far_half(0)
+                for e in outer_first[1:]:
+                    for whole in range(planes - 2):
+                        product(jnp.int32(e), whole, pl.ds(0, cols), 0, 0)
+                        results(jnp.int32(e), whole, 0, cols)
+                far_half(1)
+
+            @pl.when(t == early + 2)
+            def _():
+                far_half(2)
+
+            @pl.when(t == last_turn)
+            def _():
+                far_half(3)
+                late_result(0)
+                pl.semaphore_wait(ready.at[rounds + 1], 1)
+                far_half(4)
+                late_result(1)
+
+            product(d, c, pl.ds(at, width), i, 1)
+            results(d, c, at, width)
             return carry
 
-        def one_chunk(t, carry):
-            h, d = lax.div(t, half), first - lax.rem(t, half)
-            at = pl.multiple_of(h * width, width)
-
-            @pl.when(t == max(half * (parts - 1) - 1, 0))
-            def _():
-                for e in range(len(pairs) // 4):
-                    far_half(e)
-
-            @pl.when(t == half * (parts - 1))
-            def _():
-                for e in range(len(pairs) // 4, len(pairs) // 2):
-                    far_half(e)
-            i = (planes - 2) * parts + h
-            product(d, planes - 2, pl.ds(at, width), i, 1)
-            results(d, planes - 2, at, width)
-            return carry
-
-        lax.fori_loop(0, half * (planes - 2), whole_plane, 0)
-        lax.fori_loop(0, half * parts, one_chunk, 0)
-        pl.semaphore_wait(ready.at[rounds + 1], 1)
-        for at in range(len(pairs) // 2, held_back):
+        last_turn = early + half * parts - 1
+        lax.fori_loop(0, last_turn + 1, one, 0)
+        for at in range(5, len(pairs)):
             far_half(at)
-        near_half()
-        for at in range(max(joined, len(pairs) - held_back)):
-            if held_back + at < len(pairs):
-                far_half(held_back + at)
-            if at < joined:
-                late_result(at)
+            if at - 3 < joined:
+                late_result(at - 3)
+        for at in range(len(pairs) - 3, joined):
+            late_result(at)
         wait_bytes(op_bytes(half * half), op_send)
         wait_bytes(blocks.at[pl.ds(0, planes - 1), from_source(0), :], own_send)
         for m in range(half - 1):
@@ -400,13 +402,12 @@
         for i in range(raw):
             at = block_part(k, i)
             remote(at, at, own_send, blk_recv.at[m, i], j, centre).start()
+        remote(last_plane(k), last_plane(k), own_send, blk_recv.at[m, raw], j, centre).start()
         own_far.wait()
         own_ops.wait()
         own_part()
         part_out[...] = part[...].astype(part_out.dtype)
         for at, (d, chip) in enumerate(pairs):
-            if at == held_back:
-                remote(last_plane(k), last_plane(k), own_send, blk_recv.at[m, raw], j, centre).start()
             band = far_rows(d, 2 * chip, 2)
             remote(part_out.at[band, :], part_in.at[m, band, :], part_send, part_recv.at[m, at], j, centre).start()
         plane_entered()
@@ -488,8 +489,8 @@
 
     def body(products, operator):
         rows, planes, cols = products.shape
-        aligned = (n % 2 == 0 and n > 2 and planes > 2 and g & (g - 1) == 0 and g > 1 and rows % (g * SUBLANES) == 0
-                   and rows % LANES == 0 and cols % LANES == 0)
+        aligned = (n // 2 == 2 and n % 2 == 0 and planes > 2 and g & (g - 1) == 0 and g > 1 and rows % (g * SUBLANES) == 0
+                   and rows % LANES == 0 and cols % (2 * LANES) == 0)
         held = 2 * (products.size * (n + n // 2 + 2) + operator.size * (2 + n // 2)) + 20 * n * rows * cols
         if aligned and held < VMEM_BYTES // 2:
             return at_centres(n, g, products, operator)

time: 35.9 us -> 35.4 us (0.986)
  the two profiles are of different devices: /device:TPU:5 before, /device:TPU:7 now
where the time goes in v4:
time: 35.4 us; the launch traced here: 35.3 us
  Pallas kernels  34.4 us (97%)
  local copies, waits for them, and re-layouts  0.82 us (2%)
    pallas_call x1, Pallas kernels, at_centres(): pl.pallas_call(functools.partial(kernel, n, g, parts), out_shape=jax.Shap...  34.4 us
    unnamed x1, local copies, waits for them, and re-layouts  0.82 us

profile of v4, /device:TPU:7, one launch (start us, length us, event | category | flops | bytes accessed | tf_op | source)
XLA Modules:
  0.0 35.3 jit_solution(10234131694452764119)
XLA Ops:
  0.0 34.4 %shard_map.28 = bf16[3,48,2048]{2,1,0:T(8,128)(2,1)S(1)} custom-call(bf16[3,384,256]{2,1,0:T(8,128)(2,1)} %bitcast.3, bf16[1536,384]{1,0:T(8,128)(2,1)} %op_ref.1), custom_call_target="tpu_custom_call" | custom-call | tf_op jit(solution)/shard_map/pallas_call | solution.py:428
  34.4 0.8 %copy.4 = bf16[48,3,2048]{2,0,1:T(8,128)(2,1)} copy(bf16[48,3,2048]{2,0,1:T(8,128)(2,1)S(1)} %bitcast.2) | data formatting | bytes 1179648

commit v5 on v4

--- a/solution.py
+++ b/solution.py
@@ -321,21 +321,21 @@
             def _():
                 for e in range(3, raw):
                     forward(e)
-
-            @pl.when(t == early)
-            def _():
                 for e in outer_first[1:]:
                     share(e)
+
+            @pl.when(t == early)
+            def _():
+                for e in outer_first[1:]:
                     complete(e)
-
-            @pl.when(t == early + 1)
-            def _():
-                near_half()
-                far_half(0)
-                for e in outer_first[1:]:
                     for whole in range(planes - 2):
                         product(jnp.int32(e), whole, pl.ds(0, cols), 0, 0)
                         results(jnp.int32(e), whole, 0, cols)
+
+            @pl.when(t == early + 1)
+            def _():
+                near_half()
+                far_half(0)
                 far_half(1)
 
             @pl.when(t == early + 2)

time: 35.4 us -> 34.6 us (0.977)
  Pallas kernels: 34.4 us -> 33.5 us
    pallas_call x1, Pallas kernels: 34.4 us -> 33.5 us  [at_centres(): pl.pallas_call(functools.partial(kernel, n, g, parts), out_shape=jax.Shap...]
where the time goes in v5:
time: 34.6 us; the launch traced here: 34.3 us
  Pallas kernels  33.5 us (97%)
  local copies, waits for them, and re-layouts  0.82 us (2%)
    pallas_call x1, Pallas kernels, at_centres(): pl.pallas_call(functools.partial(kernel, n, g, parts), out_shape=jax.Shap...  33.5 us
    unnamed x1, local copies, waits for them, and re-layouts  0.82 us

profile of v5, /device:TPU:7, one launch (start us, length us, event | category | flops | bytes accessed | tf_op | source)
XLA Modules:
  0.0 34.3 jit_solution(15343989849709508273)
XLA Ops:
  0.0 33.5 %shard_map.28 = bf16[3,48,2048]{2,1,0:T(8,128)(2,1)S(1)} custom-call(bf16[3,384,256]{2,1,0:T(8,128)(2,1)} %bitcast.3, bf16[1536,384]{1,0:T(8,128)(2,1)} %op_ref.1), custom_call_target="tpu_custom_call" | custom-call | tf_op jit(solution)/shard_map/pallas_call | solution.py:428
  33.5 0.8 %copy.4 = bf16[48,3,2048]{2,0,1:T(8,128)(2,1)} copy(bf16[48,3,2048]{2,0,1:T(8,128)(2,1)S(1)} %bitcast.2) | data formatting | bytes 1179648

commit v6 on v5

--- a/solution.py
+++ b/solution.py
@@ -15,7 +15,7 @@
 
 
 def kernel(n, g, parts, p_ref, op_ref, out_ref, blocks, ops, far_ops, first_ops, passing, res, wide, part, part_out, part_in,
-           far_out, far_in, near_sum, near_out, late, terms, last, own_send, fwd_send, op_send, spread_send, res_send, part_send, far_send,
+           far_out, far_in, near_sum, near_out, late, terms, own_send, fwd_send, op_send, spread_send, res_send, part_send, far_send,
            late_send, near_send, blk_recv, op_recv, pass_recv, plane_recv, sibling_recv, out_recv, part_recv, far_recv, terms_recv, own_copy,
            ready):
     j, k = lax.axis_index("gx"), lax.axis_index("gy")
@@ -220,11 +220,11 @@
             for e in range(len(sources)):
                 enter(e, d, True)
         forward(1)
-        own_ops.wait()
-        share(first)
         forward(2)
         for i in range(3, raw):
             block_out(i)
+        own_ops.wait()
+        share(first)
         complete(first)
         if half > 1:
             pl.semaphore_wait(ready.at[rounds], half - 1)
@@ -376,8 +376,7 @@
         wait_bytes(near_out.at[pl.ds(0, rows - outrows), :], near_send)
         for b in (1, 0):
             wait_bytes(terms.at[b], terms_recv.at[b])
-        last[...] = (terms[0].astype(jnp.float32) + terms[1].astype(jnp.float32)).astype(last.dtype)
-        pltpu.make_async_copy(last, out_ref.at[planes - 1], out_recv.at[1]).start()
+        out_ref[planes - 1] = (terms[0].astype(jnp.float32) + terms[1].astype(jnp.float32)).astype(out_ref.dtype)
 
     @pl.when(jnp.logical_not(is_centre))
     def _():
@@ -417,7 +416,10 @@
         wait_bytes(part_out, part_send)
 
     wait_bytes(out_ref.at[pl.ds(0, planes - 1)], out_recv.at[0])
-    wait_bytes(out_ref.at[planes - 1], out_recv.at[1])
+
+    @pl.when(jnp.logical_not(is_centre))
+    def _():
+        wait_bytes(out_ref.at[planes - 1], out_recv.at[1])
 
 
 def at_centres(n, g, products, operator):
@@ -429,7 +431,7 @@
         functools.partial(kernel, n, g, parts),
         out_shape=jax.ShapeDtypeStruct((planes, rows // g, cols * g), jnp.bfloat16),
         in_specs=[pl.BlockSpec(memory_space=pl.ANY)] * 2,
-        out_specs=pl.BlockSpec(memory_space=pl.ANY),
+        out_specs=pl.BlockSpec(memory_space=pltpu.VMEM),
         scratch_shapes=[
             pltpu.VMEM((planes, n * rows, cols), jnp.bfloat16),
             pltpu.VMEM((half * rows, n * rows), jnp.bfloat16),
@@ -447,7 +449,6 @@
             pltpu.VMEM((rows, cols), jnp.bfloat16),
             pltpu.VMEM((half * rows, cols), jnp.bfloat16),
             pltpu.VMEM((2, rows // g, g * cols), jnp.bfloat16),
-            pltpu.VMEM((rows // g, g * cols), jnp.bfloat16),
             pltpu.SemaphoreType.DMA,
             pltpu.SemaphoreType.DMA((outer,)),
             pltpu.SemaphoreType.DMA,

time: 34.6 us -> 34.4 us (level)
  no operation moved by 1% of the time
where the time goes in v6:
time: 34.4 us; the launch traced here: 34.3 us
  Pallas kernels  33.5 us (97%)
  local copies, waits for them, and re-layouts  0.82 us (2%)
    pallas_call x1, Pallas kernels, at_centres(): pl.pallas_call(functools.partial(kernel, n, g, parts), out_shape=jax.Shap...  33.5 us
    unnamed x1, local copies, waits for them, and re-layouts  0.82 us

profile of v6, /device:TPU:7, one launch (start us, length us, event | category | flops | bytes accessed | tf_op | source)
XLA Modules:
  0.0 34.3 jit_solution(1817607078018237501)
XLA Ops:
  0.0 33.5 %shard_map.28 = bf16[3,48,2048]{2,1,0:T(8,128)(2,1)S(1)} custom-call(bf16[3,384,256]{2,1,0:T(8,128)(2,1)} %bitcast.3, bf16[1536,384]{1,0:T(8,128)(2,1)} %op_ref.1), custom_call_target="tpu_custom_call" | custom-call | tf_op jit(solution)/shard_map/pallas_call | solution.py:430
  33.5 0.8 %copy.4 = bf16[48,3,2048]{2,0,1:T(8,128)(2,1)} copy(bf16[48,3,2048]{2,0,1:T(8,128)(2,1)S(1)} %bitcast.2) | data formatting | bytes 1179648

commit v7 on v6

--- a/solution.py
+++ b/solution.py
@@ -14,10 +14,10 @@
 GRANT = 54500 * 1024
 
 
-def kernel(n, g, parts, p_ref, op_ref, out_ref, blocks, ops, far_ops, first_ops, passing, res, wide, part, part_out, part_in,
-           far_out, far_in, near_sum, near_out, late, terms, own_send, fwd_send, op_send, spread_send, res_send, part_send, far_send,
-           late_send, near_send, blk_recv, op_recv, pass_recv, plane_recv, sibling_recv, out_recv, part_recv, far_recv, terms_recv, own_copy,
-           ready):
+def kernel(n, g, parts, p_ref, op_ref, out_ref, blocks, ops, far_ops, first_ops, passing, res, wide, part, part_out,
+           part_in, far_out, far_in, near_sum, near_out, late, terms, block_send, op_send, spread_send, res_send,
+           far_send, late_send, blk_recv, op_recv, pass_recv, plane_recv, sibling_recv, out_recv, part_recv, far_recv,
+           terms_recv, own_copy, ready):
     j, k = lax.axis_index("gx"), lax.axis_index("gy")
     half = n // 2
     side = lax.div(k, half)
@@ -68,23 +68,25 @@
         start = (theirs if slot == 0 else mine).start
         return pltpu.make_async_copy(
             op_ref.at[pl.ds(pl.multiple_of(start + at.start, outrows), outrows), :], first_ops.at[slot, d],
-            own_copy.at[2 * d + slot])
-
-    own_start = pltpu.make_async_copy(
-        p_ref.at[0, :, pl.ds(0, width)], blocks.at[0, from_source(k), pl.ds(0, width)], own_copy.at[2 * half])
-    own_rest = [pltpu.make_async_copy(
-        p_ref.at[0, :, pl.ds(width, cols - width)], blocks.at[0, from_source(k), pl.ds(width, cols - width)],
-        own_copy.at[2 * half + 1])] if parts > 1 else []
-    own_rest.append(pltpu.make_async_copy(
-        p_ref.at[pl.ds(1, planes - 1)], blocks.at[pl.ds(1, planes - 1), from_source(k), :], own_copy.at[2 * half + 2]))
-    own_far = pltpu.make_async_copy(op_ref.at[theirs, :], far_ops, own_copy.at[2 * half + 3])
-    own_ops = pltpu.make_async_copy(op_ref.at[mine, :], ops.at[:, from_source(k)], own_copy.at[2 * half + 4])
+            own_copy.at[slot])
+
+    own_start = pltpu.make_async_copy(p_ref.at[0], blocks.at[0, from_source(k), :], own_copy.at[2])
+    own_rest = pltpu.make_async_copy(
+        p_ref.at[pl.ds(1, planes - 1)], blocks.at[pl.ds(1, planes - 1), from_source(k), :], own_copy.at[3])
+    own_far = pltpu.make_async_copy(op_ref.at[theirs, :], far_ops, own_copy.at[4])
+    own_ops = pltpu.make_async_copy(op_ref.at[mine, :], ops.at[:, from_source(k)], own_copy.at[4])
     for d in reversed(range(half)):
         for slot in (1, 0):
             staged(slot, d).start()
     own_start.start()
-    for rest_of in own_rest + [own_far, own_ops]:
-        rest_of.start()
+    for copy in (own_rest, own_far, own_ops):
+        copy.start()
+
+    def staged_in(slot):
+        wait_bytes(first_ops.at[slot], own_copy.at[slot])
+
+    def operator_in():
+        wait_bytes(ops.at[:, pl.ds(0, 2 * rows)], own_copy.at[4])
 
     rounds = g.bit_length() - 1
     barrier = pltpu.get_barrier_semaphore()
@@ -118,6 +120,12 @@
 
     def block_part(s, i):
         return blocks.at[lax.div(i, parts), from_source(s), lanes(i)]
+
+    def near_slot(m, i):
+        return m * (raw + 1) + i
+
+    def far_slot(m, i):
+        return (half - 1) * (raw + 1) + m * raw + i
 
     def last_plane(s):
         return blocks.at[planes - 1, from_source(s), :]
@@ -137,7 +145,6 @@
             chip = jnp.where(column == c, order[at], chip)
         return chip
 
-    held_back = half * chips // 2
     turns = [pick(at) for at in range(chips - 1)]
     outer_first = list(reversed(range(half)))
     pairs = [(d, 0) for d in outer_first[:-1]] + [(d, chip) for d in outer_first[:-1] for chip in turns]
@@ -151,20 +158,18 @@
     def _():
         def block_out(i):
             at = block_part(k, i)
-            remote(at, at, own_send, blk_recv.at[half - 1, i], j, other).start()
-
+            remote(at, at, block_send, blk_recv.at[far_slot(0, i)], j, other).start()
+
+        staged_in(0)
         for d in outer_first:
-            staged(0, d).wait()
             remote(first_ops.at[0, d], ops.at[far_rows(d, j), from_source(k)],
                    op_send, op_recv.at[half - 1, d], j, other).start()
         own_start.wait()
         block_out(0)
-        for rest_of in own_rest:
-            rest_of.wait()
         block_out(1)
-        for d in outer_first:
-            staged(1, d).wait()
-        own_far.wait()
+        staged_in(1)
+        own_rest.wait()
+        operator_in()
         own_part()
 
         def spread(e, d, at, mask):
@@ -198,8 +203,8 @@
         def forward(i):
             for m in range(half - 1):
                 at = block_part(near(m + 1), i)
-                wait_bytes(at, blk_recv.at[m, i])
-                remote(at, at, fwd_send.at[m], blk_recv.at[half + m, i], j, other).start()
+                wait_bytes(at, blk_recv.at[near_slot(m, i)])
+                remote(at, at, block_send, blk_recv.at[far_slot(m + 1, i)], j, other).start()
 
         closest, rest = range(half), range(half, 2 * half - 1)
         first = half - 1
@@ -223,7 +228,6 @@
         forward(2)
         for i in range(3, raw):
             block_out(i)
-        own_ops.wait()
         share(first)
         complete(first)
         if half > 1:
@@ -243,13 +247,13 @@
             @pl.when(d > 0)
             def _():
                 for to in range(g):
-                    remote(result(to), out_ref.at[c, :, target], res_send.at[d], out_recv.at[0], to, near(d)).start()
+                    remote(result(to), out_ref.at[c, :, target], res_send, out_recv.at[0], to, near(d)).start()
 
             @pl.when(d == 0)
             def _():
                 for mask in range(1, g):
                     to = flip(mask)
-                    remote(result(to), out_ref.at[c, :, target], res_send.at[d], out_recv.at[0], to, near(d)).start()
+                    remote(result(to), out_ref.at[c, :, target], res_send, out_recv.at[0], to, near(d)).start()
                 pltpu.make_async_copy(result(j), out_ref.at[c, :, target], out_recv.at[0]).start()
 
         def product(d, c, lane, i_first, count):
@@ -259,7 +263,7 @@
             def _():
                 for e in range(half - 1):
                     for i in range(count):
-                        wait_bytes(block_part(0, 0), blk_recv.at[half - 1 + e, i_first + i])
+                        wait_bytes(block_part(0, 0), blk_recv.at[far_slot(e, i_first + i)])
             size = lane.size
             ahead = wide.at[:, pl.ds(0, size)]
             ahead[...] = jnp.dot(ops[band, others], blocks[c, others, lane], preferred_element_type=jnp.float32)
@@ -267,14 +271,14 @@
             @pl.when(d == first)
             def _():
                 for i in range(count):
-                    wait_bytes(block_part(0, 0), blk_recv.at[2 * half - 2, i_first + i])
+                    wait_bytes(block_part(0, 0), blk_recv.at[far_slot(half - 1, i_first + i)])
             total = ahead[...] + jnp.dot(
                 ops[band, from_source(final)], blocks[c, from_source(final), lane], preferred_element_type=jnp.float32)
             res[d, c, :, lane] = total.astype(res.dtype)
 
         def near_half():
             for m in range(half - 1):
-                wait_bytes(last_plane(0), blk_recv.at[m, raw])
+                wait_bytes(last_plane(0), blk_recv.at[near_slot(m, raw)])
             near_sum[...] = jnp.dot(ops[:, mine], blocks[planes - 1, mine, :], preferred_element_type=jnp.float32)
             near_out[...] = near_sum[band_of(0), :].astype(near_out.dtype)
             target = terms.at[1, :, pl.ds(pl.multiple_of(j * cols, cols), cols)]
@@ -282,7 +286,7 @@
             def term(to):
                 return near_out.at[pl.ds(pl.multiple_of(to * outrows, outrows), outrows), :]
             for mask in reversed(range(1, g)):
-                remote(term(flip(mask)), target, near_send, terms_recv.at[1], flip(mask), k).start()
+                remote(term(flip(mask)), target, late_send, terms_recv.at[1], flip(mask), k).start()
             pltpu.make_async_copy(term(j), target, terms_recv.at[1]).start()
 
         def far_half(at):
@@ -363,17 +367,12 @@
         for at in range(len(pairs) - 3, joined):
             late_result(at)
         wait_bytes(op_bytes(half * half), op_send)
-        wait_bytes(blocks.at[pl.ds(0, planes - 1), from_source(0), :], own_send)
-        for m in range(half - 1):
-            wait_bytes(blocks.at[pl.ds(0, planes - 1), from_source(0), :], fwd_send.at[m])
-        for d in range(half):
-            sent = rows - outrows if d == 0 else rows
-            wait_bytes(res.at[d, pl.ds(0, planes - 1), pl.ds(0, sent), :], res_send.at[d])
+        wait_bytes(blocks.at[pl.ds(0, planes - 1), pl.ds(0, half * rows), :], block_send)
+        wait_bytes(blocks.at[pl.ds(0, planes - 1), pl.ds(0, half * rows - outrows), :], res_send)
         for e in range(len(sources)):
             wait_bytes(op_bytes(half * (g - 1)), spread_send.at[e])
         wait_bytes(far_out, far_send)
-        wait_bytes(late.at[pl.ds(0, (half - 1) * rows), :], late_send)
-        wait_bytes(near_out.at[pl.ds(0, rows - outrows), :], near_send)
+        wait_bytes(late.at[pl.ds(0, half * rows - outrows), :], late_send)
         for b in (1, 0):
             wait_bytes(terms.at[b], terms_recv.at[b])
         out_ref[planes - 1] = (terms[0].astype(jnp.float32) + terms[1].astype(jnp.float32)).astype(out_ref.dtype)
@@ -383,37 +382,36 @@
         m = away - 1
 
         def op_in(d):
-            staged(1, d).wait()
             remote(first_ops.at[1, d], ops.at[near_rows(d, j), from_source(k)],
                    op_send, op_recv.at[m, d], j, centre).start()
 
         def op_past(d):
-            staged(0, d).wait()
             remote(first_ops.at[0, d], passing.at[m, d], op_send, pass_recv.at[m, d], j, centre).start()
 
+        staged_in(1)
         op_in(half - 1)
+        staged_in(0)
         for d in outer_first:
             op_past(d)
         for d in outer_first[1:]:
             op_in(d)
-        for rest_of in [own_start] + own_rest:
-            rest_of.wait()
+        own_start.wait()
+        own_rest.wait()
         for i in range(raw):
             at = block_part(k, i)
-            remote(at, at, own_send, blk_recv.at[m, i], j, centre).start()
-        remote(last_plane(k), last_plane(k), own_send, blk_recv.at[m, raw], j, centre).start()
-        own_far.wait()
-        own_ops.wait()
+            remote(at, at, block_send, blk_recv.at[near_slot(m, i)], j, centre).start()
+        remote(last_plane(k), last_plane(k), block_send, blk_recv.at[near_slot(m, raw)], j, centre).start()
+        operator_in()
         own_part()
         part_out[...] = part[...].astype(part_out.dtype)
         for at, (d, chip) in enumerate(pairs):
             band = far_rows(d, 2 * chip, 2)
-            remote(part_out.at[band, :], part_in.at[m, band, :], part_send, part_recv.at[m, at], j, centre).start()
+            remote(part_out.at[band, :], part_in.at[m, band, :], far_send, part_recv.at[m, at], j, centre).start()
         plane_entered()
         signal(ready.at[rounds], j, centre)
         wait_bytes(op_bytes(2 * half), op_send)
-        wait_bytes(blocks.at[:, from_source(0), :], own_send)
-        wait_bytes(part_out, part_send)
+        wait_bytes(blocks.at[:, from_source(0), :], block_send)
+        wait_bytes(part_out, far_send)
 
     wait_bytes(out_ref.at[pl.ds(0, planes - 1)], out_recv.at[0])
 
@@ -450,15 +448,12 @@
             pltpu.VMEM((half * rows, cols), jnp.bfloat16),
             pltpu.VMEM((2, rows // g, g * cols), jnp.bfloat16),
             pltpu.SemaphoreType.DMA,
-            pltpu.SemaphoreType.DMA((outer,)),
             pltpu.SemaphoreType.DMA,
             pltpu.SemaphoreType.DMA((roles,)),
-            pltpu.SemaphoreType.DMA((half,)),
             pltpu.SemaphoreType.DMA,
             pltpu.SemaphoreType.DMA,
             pltpu.SemaphoreType.DMA,
-            pltpu.SemaphoreType.DMA,
-            pltpu.SemaphoreType.DMA((roles, raw + 1)),
+            pltpu.SemaphoreType.DMA((outer * (raw + 1) + half * raw,)),
             pltpu.SemaphoreType.DMA((roles, half)),
             pltpu.SemaphoreType.DMA((outer, half)),
             pltpu.SemaphoreType.DMA((roles, half)),
@@ -467,7 +462,7 @@
             pltpu.SemaphoreType.DMA((outer, half * g // 2)),
             pltpu.SemaphoreType.DMA((outer * g // 2,)),
             pltpu.SemaphoreType.DMA((2,)),
-            pltpu.SemaphoreType.DMA((2 * half + 5,)),
+            pltpu.SemaphoreType.DMA((5,)),
             pltpu.SemaphoreType.REGULAR((g.bit_length() + 1,)),
         ],
         compiler_params=pltpu.CompilerParams(
@@ -490,7 +485,7 @@
 
     def body(products, operator):
         rows, planes, cols = products.shape
-        aligned = (n // 2 == 2 and n % 2 == 0 and planes > 2 and g & (g - 1) == 0 and g > 1 and rows % (g * SUBLANES) == 0
+        aligned = (n // 2 == 2 and n % 2 == 0 and planes > 2 and g & (g - 1) == 0 and g > 4 and rows % (g * SUBLANES) == 0
                    and rows % LANES == 0 and cols % (2 * LANES) == 0)
         held = 2 * (products.size * (n + n // 2 + 2) + operator.size * (2 + n // 2)) + 20 * n * rows * cols
         if aligned and held < VMEM_BYTES // 2:

time: 34.4 us -> 34.3 us (level)
  no operation moved by 1% of the time
where the time goes in v7:
time: 34.3 us; the launch traced here: 34.2 us
  Pallas kernels  33.4 us (97%)
  local copies, waits for them, and re-layouts  0.82 us (2%)
    pallas_call x1, Pallas kernels, at_centres(): pl.pallas_call(functools.partial(kernel, n, g, parts), out_shape=jax.Shap...  33.4 us
    unnamed x1, local copies, waits for them, and re-layouts  0.82 us

profile of v7, /device:TPU:7, one launch (start us, length us, event | category | flops | bytes accessed | tf_op | source)
XLA Modules:
  0.0 34.2 jit_solution(14545959319111337296)
XLA Ops:
  0.0 33.4 %shard_map.28 = bf16[3,48,2048]{2,1,0:T(8,128)(2,1)S(1)} custom-call(bf16[3,384,256]{2,1,0:T(8,128)(2,1)} %bitcast.3, bf16[1536,384]{1,0:T(8,128)(2,1)} %op_ref.1), custom_call_target="tpu_custom_call" | custom-call | tf_op jit(solution)/shard_map/pallas_call | solution.py:428
  33.4 0.8 %copy.4 = bf16[48,3,2048]{2,0,1:T(8,128)(2,1)} copy(bf16[48,3,2048]{2,0,1:T(8,128)(2,1)S(1)} %bitcast.2) | data formatting | bytes 1179648

commit v8 on v7

--- a/solution.py
+++ b/solution.py
@@ -63,6 +63,21 @@
     def op_bytes(pieces):
         return ops.at[pl.ds(0, pieces * outrows), pl.ds(0, rows)]
 
+    rounds = g.bit_length() - 1
+    barrier = pltpu.get_barrier_semaphore()
+
+    def signal(sem, gx, gy):
+        pl.semaphore_signal(sem, inc=1, device_id=(gx, gy), device_id_type=MESH)
+
+    @pl.when(is_centre)
+    def _():
+        signal(barrier, j, other)
+        for d in range(1, half):
+            signal(barrier, j, near(d))
+
+    for b in range(rounds):
+        signal(barrier, flip(1 << b), k)
+
     def staged(slot, d):
         at = far_rows(d, j) if slot == 0 else near_rows(d, j)
         start = (theirs if slot == 0 else mine).start
@@ -87,21 +102,6 @@
 
     def operator_in():
         wait_bytes(ops.at[:, pl.ds(0, 2 * rows)], own_copy.at[4])
-
-    rounds = g.bit_length() - 1
-    barrier = pltpu.get_barrier_semaphore()
-
-    def signal(sem, gx, gy):
-        pl.semaphore_signal(sem, inc=1, device_id=(gx, gy), device_id_type=MESH)
-
-    for b in range(rounds):
-        signal(barrier, flip(1 << b), k)
-
-    @pl.when(is_centre)
-    def _():
-        signal(barrier, j, other)
-        for d in range(1, half):
-            signal(barrier, j, near(d))
 
     pl.semaphore_wait(barrier, rounds + 1)
 

time: 34.3 us -> 34.3 us (level)
  no operation moved by 1% of the time
where the time goes in v8:
time: 34.3 us; the launch traced here: 34.2 us
  Pallas kernels  33.4 us (97%)
  local copies, waits for them, and re-layouts  0.82 us (2%)
    pallas_call x1, Pallas kernels, at_centres(): pl.pallas_call(functools.partial(kernel, n, g, parts), out_shape=jax.Shap...  33.4 us
    unnamed x1, local copies, waits for them, and re-layouts  0.82 us

profile of v8, /device:TPU:7, one launch (start us, length us, event | category | flops | bytes accessed | tf_op | source)
XLA Modules:
  0.0 34.2 jit_solution(17305501532556708478)
XLA Ops:
  0.0 33.4 %shard_map.28 = bf16[3,48,2048]{2,1,0:T(8,128)(2,1)S(1)} custom-call(bf16[3,384,256]{2,1,0:T(8,128)(2,1)} %bitcast.3, bf16[1536,384]{1,0:T(8,128)(2,1)} %op_ref.1), custom_call_target="tpu_custom_call" | custom-call | tf_op jit(solution)/shard_map/pallas_call | solution.py:428
  33.4 0.8 %copy.4 = bf16[48,3,2048]{2,0,1:T(8,128)(2,1)} copy(bf16[48,3,2048]{2,0,1:T(8,128)(2,1)S(1)} %bitcast.2) | data formatting | bytes 1179648

commit v9 on v8

--- a/solution.py
+++ b/solution.py
@@ -349,10 +349,6 @@
             @pl.when(t == last_turn)
             def _():
                 far_half(3)
-                late_result(0)
-                pl.semaphore_wait(ready.at[rounds + 1], 1)
-                far_half(4)
-                late_result(1)
 
             product(d, c, pl.ds(at, width), i, 1)
             results(d, c, at, width)
@@ -360,6 +356,10 @@
 
         last_turn = early + half * parts - 1
         lax.fori_loop(0, last_turn + 1, one, 0)
+        late_result(0)
+        pl.semaphore_wait(ready.at[rounds + 1], 1)
+        far_half(4)
+        late_result(1)
         for at in range(5, len(pairs)):
             far_half(at)
             if at - 3 < joined:

time: 34.3 us -> 34.3 us (level)
  no operation moved by 1% of the time
where the time goes in v9:
time: 34.3 us; the launch traced here: 34.2 us
  Pallas kernels  33.4 us (97%)
  local copies, waits for them, and re-layouts  0.82 us (2%)
    pallas_call x1, Pallas kernels, at_centres(): pl.pallas_call(functools.partial(kernel, n, g, parts), out_shape=jax.Shap...  33.4 us
    unnamed x1, local copies, waits for them, and re-layouts  0.82 us

profile of v9, /device:TPU:7, one launch (start us, length us, event | category | flops | bytes accessed | tf_op | source)
XLA Modules:
  0.0 34.2 jit_solution(4650299653881362456)
XLA Ops:
  0.0 33.4 %shard_map.28 = bf16[3,48,2048]{2,1,0:T(8,128)(2,1)S(1)} custom-call(bf16[3,384,256]{2,1,0:T(8,128)(2,1)} %bitcast.3, bf16[1536,384]{1,0:T(8,128)(2,1)} %op_ref.1), custom_call_target="tpu_custom_call" | custom-call | tf_op jit(solution)/shard_map/pallas_call | solution.py:428
  33.4 0.8 %copy.4 = bf16[48,3,2048]{2,0,1:T(8,128)(2,1)} copy(bf16[48,3,2048]{2,0,1:T(8,128)(2,1)S(1)} %bitcast.2) | data formatting | bytes 1179648

commit v10 on v9

--- a/solution.py
+++ b/solution.py
@@ -182,7 +182,7 @@
 
         def enter(e, d, everywhere):
             wait_bytes(op_bytes(1), op_recv.at[e, d])
-            for mask in (distant if everywhere else []) + adjacent:
+            for mask in [1] + (distant if everywhere else []) + adjacent[:-1]:
                 spread(e, d, j, mask)
 
         def share(d):

time: 34.3 us -> 34.3 us (level)
  no operation moved by 1% of the time
where the time goes in v10:
time: 34.3 us; the launch traced here: 34.2 us
  Pallas kernels  33.4 us (97%)
  local copies, waits for them, and re-layouts  0.82 us (2%)
    pallas_call x1, Pallas kernels, at_centres(): pl.pallas_call(functools.partial(kernel, n, g, parts), out_shape=jax.Shap...  33.4 us
    unnamed x1, local copies, waits for them, and re-layouts  0.82 us

profile of v10, /device:TPU:7, one launch (start us, length us, event | category | flops | bytes accessed | tf_op | source)
XLA Modules:
  0.0 34.2 jit_solution(14874956755046904850)
XLA Ops:
  0.0 33.4 %shard_map.28 = bf16[3,48,2048]{2,1,0:T(8,128)(2,1)S(1)} custom-call(bf16[3,384,256]{2,1,0:T(8,128)(2,1)} %bitcast.3, bf16[1536,384]{1,0:T(8,128)(2,1)} %op_ref.1), custom_call_target="tpu_custom_call" | custom-call | tf_op jit(solution)/shard_map/pallas_call | solution.py:428
  33.4 0.8 %copy.4 = bf16[48,3,2048]{2,0,1:T(8,128)(2,1)} copy(bf16[48,3,2048]{2,0,1:T(8,128)(2,1)S(1)} %bitcast.2) | data formatting | bytes 1179648

commit v11 on v10

--- a/solution.py
+++ b/solution.py
@@ -149,7 +149,7 @@
     outer_first = list(reversed(range(half)))
     pairs = [(d, 0) for d in outer_first[:-1]] + [(d, chip) for d in outer_first[:-1] for chip in turns]
     joined = len(pairs)
-    pairs += [(0, chip) for chip in [0] + turns]
+    pairs += [(0, chip) for chip in turns[:1] + [0] + turns[1:]]
 
     def own_part():
         part[...] = jnp.dot(far_ops[...], last_plane(k)[...], preferred_element_type=jnp.float32)

time: 34.3 us -> 34.3 us (level)
  no operation moved by 1% of the time
where the time goes in v11:
time: 34.3 us; the launch traced here: 34.2 us
  Pallas kernels  33.4 us (97%)
  local copies, waits for them, and re-layouts  0.82 us (2%)
    pallas_call x1, Pallas kernels, at_centres(): pl.pallas_call(functools.partial(kernel, n, g, parts), out_shape=jax.Shap...  33.4 us
    unnamed x1, local copies, waits for them, and re-layouts  0.82 us

profile of v11, /device:TPU:7, one launch (start us, length us, event | category | flops | bytes accessed | tf_op | source)
XLA Modules:
  0.0 34.2 jit_solution(16891441706423496130)
XLA Ops:
  0.0 33.4 %shard_map.28 = bf16[3,48,2048]{2,1,0:T(8,128)(2,1)S(1)} custom-call(bf16[3,384,256]{2,1,0:T(8,128)(2,1)} %bitcast.3, bf16[1536,384]{1,0:T(8,128)(2,1)} %op_ref.1), custom_call_target="tpu_custom_call" | custom-call | tf_op jit(solution)/shard_map/pallas_call | solution.py:428
  33.4 0.8 %copy.4 = bf16[48,3,2048]{2,0,1:T(8,128)(2,1)} copy(bf16[48,3,2048]{2,0,1:T(8,128)(2,1)S(1)} %bitcast.2) | data formatting | bytes 1179648
